TPU v7x, 32 devices: a whole 2x2x4 slice. The times are simulated.
32 devices in a mesh: row: 4 (over y, x), col: 8 (over z, core).
Axes of the slice: x: 2, y: 2, z: 4, core: 2. Of those that a mesh axis runs over, the one named last changes fastest.
Arguments:
- basis: bfloat16 [40, 131072], P(None, ('row', 'col'))
- expand: float32 [3, 8, 40], replicated, may hold values from -1 to 1
- tiles: bfloat16 [3, 3072, 128, 128], P(None, ('row', 'col')), may hold values from -0.3125 to 0.3125
- tile_rows: int32 [3072], P(('row', 'col')), may hold values from 0 to 255, as said below
- tile_cols: int32 [3072], P(('row', 'col')), may hold values from 0 to 127
Outputs:
- new_block: float32 [8, 131072], P(None, ('row', 'col'))
- coefficients: float32 [8, 40], replicated
- factor: float32 [8, 8], replicated
Inputs may be any that keep to these rules, and one draw needn't show every extreme that they name: `tile_rows`: each device's 96 tiles come in 8 runs of 12; the row tiles of run k are 12 distinct values from k * 32 to (k + 1) * 32 - 1.
All inputs are finite; a program needn't handle non-finite values.
Results may differ from a plain program's by a relative error of at most 0.0054.
Values may be sent and summed in bfloat16 or wider, within the bound.
No kernel may reach another device: no remote copies, remote signals or barrier semaphores. Data moves between devices by JAX's collectives and lax.ppermute only.
A program may use at most 64 MiB of HBM per device.

v0:
```python
import functools
import math

import jax
import jax.numpy as jnp
from jax import lax
from jax.experimental import pallas as pl
from jax.experimental.pallas import tpu as pltpu
from jax.sharding import PartitionSpec as P


F32 = jnp.float32
BF16 = jnp.bfloat16
HALF = 64


def contract_lanes(a, b):
    return lax.dot_general(a, b, (((1,), (1,)), ((), ())), preferred_element_type=F32)


def split3(value):
    high = value.astype(BF16).astype(F32)
    rest = value - high
    middle = rest.astype(BF16).astype(F32)
    return high, middle, rest - middle


def series_kernel(region, tile, extra, basis_ref, expand_ref, out_ref, scratch, here, small, sems):
    rows, krylov = expand_ref.shape
    copies = [
        pltpu.make_async_copy(basis_ref, here, sems.at[0]),
        pltpu.make_async_copy(expand_ref, small, sems.at[1]),
    ]
    for copy in copies:
        copy.start()
    scratch[...] = jnp.zeros_like(scratch)
    for copy in copies:
        copy.wait()
    basis = here[...]
    parts = jnp.concatenate(split3(small[...]), axis=0).astype(BF16)
    wide = jnp.dot(parts, basis, preferred_element_type=F32)
    series = (wide[:rows] + wide[rows : 2 * rows] + wide[2 * rows :]).astype(BF16)
    for t in range(region):
        out_ref[t] = series[:, t * tile : (t + 1) * tile]
    local = contract_lanes(basis, basis)
    high = local.astype(BF16).astype(F32)
    scratch[:krylov, :krylov] = high
    scratch[:krylov, HALF : HALF + krylov] = local - high
    for e in range(extra):
        out_ref[region + e] = scratch[e * rows : (e + 1) * rows, :].astype(BF16)


def share_correlation(sizes, gathered_ref, scratch, slices):
    row_count, region, extra, krylov, _, _, share = sizes
    rows, tile = gathered_ref.shape[2:]
    total = jnp.zeros((extra * rows, tile), F32)
    for r in range(row_count):
        total += jnp.concatenate(
            [gathered_ref[r, region + e].astype(F32) for e in range(extra)], axis=0
        )
    scratch[...] = jnp.zeros_like(scratch)
    merged = total[:krylov, :krylov] + total[:krylov, HALF : HALF + krylov]
    high = merged.astype(BF16).astype(F32)
    scratch[:krylov, :krylov] = high
    scratch[:krylov, HALF : HALF + krylov] = merged - high
    slices[...] = jnp.zeros_like(slices)
    for c in range(slices.shape[0]):
        if c * share < krylov:
            slices[c, :share, :] = scratch[c * share : (c + 1) * share, :]


def tile_kernel(sizes, core, distances, first, cols_ref, rows_ref, gathered_ref, tiles_ref, *refs):
    _, region, _, _, cap, vectors, _ = sizes
    tile = tiles_ref.shape[2]
    position = lax.axis_index("col")
    if first:
        out_ref, slices, scratch = refs
        share_correlation(sizes, gathered_ref, scratch, slices)
    else:
        slices, out_ref = refs
    lane = lax.broadcasted_iota(jnp.int32, (8, tile), 1)
    sublane = lax.broadcasted_iota(jnp.int32, (8, tile), 0)
    slot = lane // vectors
    inner = lane - slot * vectors

    def column(t):
        c = cols_ref[pl.ds(t, 1), :1][0, 0]
        r = lax.div(c, region)
        x = gathered_ref[r, c - r * region]
        return [x[m * vectors : (m + 1) * vectors] for m in range(3)]

    def weights(m, t):
        return tiles_ref[m, pl.ds(t, 2)].reshape(2 * tile, tile)

    def side(a, b):
        return jnp.concatenate([a, b], axis=1)

    def block(distance, place):
        target = (position ^ (2 * distance)) ^ core
        base = target * cap

        def store(p, out):
            pair = jnp.concatenate([out[:vectors, :tile], out[vectors:, tile:]], axis=0)
            out_ref[place, 2 * p * vectors : (2 * p + 2) * vectors, :] = pair.astype(BF16)

        pairs = []
        for p in range(cap // 2):
            t = base + 2 * p
            x0, x1 = column(t), column(t + 1)
            lhs = jnp.concatenate([side(x0[0], x0[1]), side(x1[0], x1[1])], axis=0)
            rhs = side(weights(0, t), weights(1, t))
            third = jnp.concatenate([x0[2], x1[2]], axis=0)
            pairs.append((p, contract_lanes(lhs, rhs), third, weights(2, t)))
        while len(pairs) > 1:
            (p, out_p, x_p, w_p), (q, out_q, x_q, w_q) = pairs[:2]
            pairs = pairs[2:]
            zero = jnp.zeros_like(x_p)
            lhs = jnp.concatenate([side(x_p, zero), side(zero, x_q)], axis=0)
            both = contract_lanes(lhs, side(w_p, w_q))
            store(p, out_p + both[: 2 * vectors])
            store(q, out_q + both[2 * vectors :])
        for p, out_p, x_p, w_p in pairs:
            store(p, out_p + contract_lanes(x_p, w_p))
        code = jnp.full((8, tile), -1, jnp.int32)
        for s in range(cap):
            code = jnp.where(
                slot == s, (rows_ref[pl.ds(base + s, 1), :] - target * region) * vectors + inner, code
            )
        last = jnp.where(sublane == 7, code.astype(F32), slices[target])
        out_ref[place, cap * vectors : (cap + 1) * vectors, :] = last.astype(BF16)

    for place, distance in enumerate(distances):
        block(distance, place)


def merge_kernel(sizes, basis_ref, *refs):
    region, krylov, cap, vectors, each = sizes
    blocks, (applied_ref, packet_ref, scratch) = refs[:-3], refs[-3:]
    tile = applied_ref.shape[1] // region
    total = jnp.zeros((region * vectors, tile), F32)
    small = jnp.zeros((vectors, tile), F32)
    place = lax.broadcasted_iota(jnp.int32, (region * vectors, tile), 0).astype(F32)
    span = (cap + 1) * vectors
    for ref in blocks:
        for part in range(ref.shape[0]):
            piece = ref[part]
            last = piece[cap * vectors :].astype(F32)
            small += last
            onehot = jnp.where(place == last[7:8, :], 1.0, 0.0).astype(BF16)
            total += jnp.dot(onehot[:, :span], piece, preferred_element_type=F32)
    for t in range(region):
        applied_ref[:, t * tile : (t + 1) * tile] = total[t * vectors : (t + 1) * vectors]
    applied = applied_ref[...]
    high, middle, _ = split3(applied)
    lhs = jnp.concatenate([high, middle], axis=0).astype(BF16)
    inner = contract_lanes(lhs, basis_ref[...])
    raw = inner[:vectors] + inner[vectors:]
    cross = contract_lanes(lhs, lhs)
    energy = (cross[:vectors, :vectors] + cross[vectors:, vectors:]) + (
        cross[:vectors, vectors:] + cross[vectors:, :vectors]
    )
    low_half = pltpu.roll(small, tile - HALF, 1)
    lane = lax.broadcasted_iota(jnp.int32, (vectors, tile), 1)
    sublane = lax.broadcasted_iota(jnp.int32, (vectors, tile), 0)
    scratch[...] = jnp.zeros_like(scratch)
    scratch[:vectors, :] = jnp.where(lane < krylov, small + low_half, 0.0)
    used = krylov + vectors
    width = HALF - used
    packet = jnp.concatenate([raw, energy, jnp.zeros((vectors, tile - used), F32)], axis=1)
    first_row = lax.axis_index("row") * each
    pieces = -(-krylov // width)
    for i in range(each):
        row = scratch[pl.ds(first_row + i, 1), :]
        for p in range(pieces):
            moved = pltpu.roll(row, (used - p * width) % tile, 1)
            here = (sublane == i * pieces + p) & (lane >= used) & (lane < HALF)
            packet = jnp.where(here, moved, packet)
    folded = jnp.where(
        lane[: vectors // 2] < HALF,
        packet[: vectors // 2],
        pltpu.roll(packet, HALF, 1)[vectors // 2 :],
    )
    packet_ref[...] = jnp.broadcast_to(folded[None], packet_ref.shape)


def tree_sum(values):
    while len(values) > 1:
        values = [sum(values[i : i + 2]) for i in range(0, len(values), 2)]
    return values[0]


def finish_kernel(
    sizes, packets_ref, applied_ref, basis_ref, new_ref, coefficients_ref, factor_ref, scratch
):
    krylov, vectors, share, each, col_count, entries = sizes
    inverse_root = 1.0 / math.sqrt(entries)
    highest = lax.Precision.HIGHEST
    devices, half, tile = packets_ref.shape
    folded = tree_sum([packets_ref[d] for d in range(devices)])
    total = jnp.concatenate([folded, pltpu.roll(folded, HALF, 1)], axis=0)
    used = krylov + vectors
    width = HALF - used
    pieces = -(-krylov // width)
    lanes = lax.broadcasted_iota(jnp.int32, (devices, tile), 1)
    for i in range(each):
        found = jnp.zeros((devices, tile), F32)
        for p in range(pieces):
            n = i * pieces + p
            start = used + (n // half) * HALF
            moved = pltpu.roll(packets_ref[:, n % half, :], (p * width - start) % tile, 1)
            found = jnp.where((lanes >= p * width) & (lanes < (p + 1) * width), moved, found)
        for d in range(devices):
            r, c = divmod(d, col_count)
            row = c * share + r * each + i
            if r * each + i < share and row < krylov:
                scratch[row : row + 1, :] = found[d : d + 1]
    correlation = scratch[:krylov, :krylov] * (1.0 / entries)
    first = total[:, :krylov] * inverse_root
    energy = total[:, krylov : krylov + vectors]
    dot = functools.partial(jnp.dot, precision=highest, preferred_element_type=F32)
    across = functools.partial(
        lax.dot_general,
        dimension_numbers=(((1,), (1,)), ((), ())),
        precision=highest,
        preferred_element_type=F32,
    )
    coefficients = first + (first - dot(first, correlation))
    coefficients_ref[...] = coefficients
    parts = jnp.concatenate(split3(coefficients * inverse_root), axis=0).astype(BF16)
    wide = jnp.dot(parts, basis_ref[...], preferred_element_type=F32)
    cleaned = applied_ref[...] - (
        wide[:vectors] + (wide[vectors : 2 * vectors] + wide[2 * vectors :])
    )
    mixed = across(first, coefficients)
    mixed_t = across(coefficients, first)
    curved = across(dot(coefficients, correlation), coefficients)
    gram = (energy - mixed - mixed_t + curved) * (1.0 / entries)
    columns = [jnp.broadcast_to(gram[:, j : j + 1], (vectors, tile)) for j in range(vectors)]
    sublane = lax.broadcasted_iota(jnp.int32, (vectors, tile), 0)
    lane = lax.broadcasted_iota(jnp.int32, (vectors, tile), 1)
    factor = jnp.zeros((vectors, tile), F32)
    length = cleaned.shape[1]
    for j in range(vectors):
        inverse = lax.rsqrt(columns[j][j : j + 1, :])
        column = jnp.where(sublane >= j, columns[j] * inverse, 0.0)
        factor = jnp.where(lane == j, column, factor)
        for k in range(j + 1, vectors):
            columns[k] = columns[k] - column * column[k : k + 1, :]
        below = jnp.where(sublane > j, column, 0.0)
        pieces = []
        for t in range(length // tile):
            piece = cleaned[:, t * tile : (t + 1) * tile]
            row = piece[j : j + 1, :] * inverse
            pieces.append(jnp.where(sublane == j, row, piece - below * row))
        cleaned = jnp.concatenate(pieces, axis=1)
    factor_ref[...] = factor[:, :vectors]
    new_ref[...] = cleaned


def shards(basis, expand, tiles, tile_rows, tile_cols):
    row_count = lax.axis_size("row")
    col_count = lax.axis_size("col")
    krylov, length = basis.shape
    tile = tiles.shape[2]
    vectors = expand.shape[1]
    rows = expand.shape[0] * vectors
    region = length // tile
    devices = row_count * col_count
    entries = length * devices
    cap = tiles.shape[1] // col_count
    extra = -(-krylov // rows)
    share = -(-krylov // col_count)
    each = -(-share // row_count)
    span = (cap + 1) * vectors
    assert krylov + vectors < HALF and share < 8 and region * vectors <= 256
    assert each * -(-krylov // (HALF - krylov - vectors)) <= vectors and cap % 2 == 0
    vmem = pl.BlockSpec(memory_space=pltpu.VMEM)
    smem = pl.BlockSpec(memory_space=pltpu.SMEM)
    hbm = pl.BlockSpec(memory_space=pltpu.HBM)

    series = pl.pallas_call(
        functools.partial(series_kernel, region, tile, extra),
        out_shape=jax.ShapeDtypeStruct((region + extra, rows, tile), BF16),
        in_specs=[hbm, hbm],
        out_specs=vmem,
        scratch_shapes=[
            pltpu.VMEM((extra * rows, tile), F32),
            pltpu.VMEM(basis.shape, BF16),
            pltpu.VMEM((rows, krylov), F32),
            pltpu.SemaphoreType.DMA((2,)),
        ],
        cost_estimate=pl.CostEstimate(flops=10**10, bytes_accessed=10**7, transcendentals=0),
        compiler_params=pltpu.CompilerParams(vmem_limit_bytes=4 << 20),
        name="series",
    )(pltpu.with_memory_space_constraint(basis, pltpu.HBM), pltpu.with_memory_space_constraint(expand.reshape(rows, krylov), pltpu.HBM))
    gathered = lax.all_gather(series, "row", axis=0)
    half = col_count // 2
    sizes = (row_count, region, extra, krylov, cap, vectors, share)
    table = jax.ShapeDtypeStruct((col_count, 8, tile), F32)

    wide_cols = jnp.broadcast_to(tile_cols[:, None], (tile_cols.shape[0], tile))
    wide_rows = jnp.broadcast_to(tile_rows[:, None], (tile_cols.shape[0], tile))

    def products(core, distances, *slices):
        first = not slices
        outgoing = jax.ShapeDtypeStruct((len(distances), span, tile), BF16)
        return pl.pallas_call(
            functools.partial(tile_kernel, sizes, core, distances, first),
            out_shape=(outgoing, table) if first else outgoing,
            in_specs=[vmem, vmem, vmem, vmem] + [vmem] * len(slices),
            out_specs=(vmem, vmem) if first else vmem,
            scratch_shapes=[
                pltpu.VMEM((max(extra * rows, share * col_count), tile), F32)
            ] * first,
            cost_estimate=pl.CostEstimate(
                flops=5 * 10**9, bytes_accessed=10**7, transcendentals=0
            ),
            compiler_params=pltpu.CompilerParams(vmem_limit_bytes=16 << 20),
            name="products",
        )(wide_cols, wide_rows, gathered, tiles, *slices)

    apart = tuple(range(half - 1, 0, -1))
    swap = [(i, i ^ 1) for i in range(col_count)]
    other, slices = products(1, apart + (0,))
    partner = lax.ppermute(other, "col", swap)
    mine = products(0, apart, slices)
    own = products(0, (0,), slices)
    blocks = [own, partner[half - 1 :]]
    for place, distance in enumerate(apart):
        moves = [(i, i ^ (2 * distance)) for i in range(col_count)]
        pair = jnp.stack([mine[place], partner[place]])
        blocks.append(lax.ppermute(pair, "col", moves))
    applied, packet = pl.pallas_call(
        functools.partial(merge_kernel, (region, krylov, cap, vectors, each)),
        out_shape=(
            jax.ShapeDtypeStruct((vectors, length), F32),
            jax.ShapeDtypeStruct((devices, vectors // 2, tile), F32),
        ),
        in_specs=[vmem] * (1 + len(blocks)),
        out_specs=(vmem, vmem),
        scratch_shapes=[pltpu.VMEM((max(8, row_count * each), tile), F32)],
        compiler_params=pltpu.CompilerParams(vmem_limit_bytes=8 << 20),
        name="merge",
    )(basis, *blocks)
    packets = lax.all_to_all(packet, ("row", "col"), 0, 0, tiled=True)
    return pl.pallas_call(
        functools.partial(finish_kernel, (krylov, vectors, share, each, col_count, entries)),
        out_shape=(
            jax.ShapeDtypeStruct((vectors, length), F32),
            jax.ShapeDtypeStruct((vectors, krylov), F32),
            jax.ShapeDtypeStruct((vectors, vectors), F32),
        ),
        in_specs=[vmem] * 3,
        out_specs=(vmem,) * 3,
        scratch_shapes=[pltpu.VMEM((share * col_count, tile), F32)],
        compiler_params=pltpu.CompilerParams(vmem_limit_bytes=4 << 20),
        name="finish",
    )(packets, applied, basis)


def solution(mesh):
    return jax.shard_map(
        shards,
        mesh=mesh,
        in_specs=(
            P(None, ("row", "col")),
            P(),
            P(None, ("row", "col"), None, None),
            P(("row", "col")),
            P(("row", "col")),
        ),
        out_specs=(P(None, ("row", "col")), P(), P()),
        check_vma=False,
    )
```

profile of v0, /device:TPU:0, one launch (start us, length us, event | category | flops | bytes accessed | tf_op | source)
XLA Modules:
  0.0 41.4 jit_solution(13424396570161934733)
XLA Ops:
  0.6 0.0 copy-start.2
  0.6 0.0 copy-start.3
  0.7 0.0 copy-start.1
  0.7 1.6 %series.1 = bf16[34,24,128]{2,1,0:T(8,128)(2,1)S(1)} custom-call(bf16[40,4096]{1,0:T(8,128)(2,1)} %basis_ref.5, f32[24,40]{1,0:T(8,128)} %bitcast.5), custom_call_target="tpu_custom_call" | custom-call | flops 10000000000 | bytes 10000000 | tf_op jit(solution)/shard_map/series/pallas_call | solution.py:281
  2.3 13.7 %all-gather = bf16[136,24,128]{2,1,0:T(8,128)(2,1)S(1)} all-gather(bf16[34,24,128]{2,1,0:T(8,128)(2,1)S(1)} %series.1), channel_id=2, replica_groups=mesh['row'=4,'col'=8] {'row'}, dimensions={0}, use_global_device_ids=true | all-gather | bytes 1044480 | tf_op jit(solution)/shard_map/all_gather | solution.py:296
  16.0 0.0 copy-done.2
  16.0 0.1 broadcast_in_dim.5.rows_ref
  16.0 0.0 copy-done.3
  16.0 0.1 broadcast_in_dim.4.cols_ref
  16.1 1.4 %products.3 = (bf16[4,104,128]{2,1,0:T(8,128)(2,1)S(1)}, f32[8,8,128]{2,1,0:T(8,128)S(1)}) custom-call(s32[96,128]{1,0:T(8,128)S(1)} %broadcast_in_dim.4.cols_ref, s32[96,128]{1,0:T(8,128)S(1)} %broadcast_in_dim.5.rows_ref, bf16[4,34,24,128]{3,2,1,0:T(8,128)(2,1)S(1)} %bitcast.2, bf16[3,96,128,128]{3,2,1,0:T(8,128)(2,1)S(1)} %copy-done.1), custom_call_target="tpu_custom_call" | custom-call | flops 5000000000 | bytes 10000000 | tf_op jit(solution)/shard_map/products/pallas_call | solution.py:307
  17.6 0.0 collective-permute-start
  17.6 1.1 %products.5 = bf16[3,104,128]{2,1,0:T(8,128)(2,1)S(1)} custom-call(s32[96,128]{1,0:T(8,128)S(1)} %broadcast_in_dim.4.cols_ref, s32[96,128]{1,0:T(8,128)S(1)} %broadcast_in_dim.5.rows_ref, bf16[4,34,24,128]{3,2,1,0:T(8,128)(2,1)S(1)} %bitcast.3, bf16[3,96,128,128]{3,2,1,0:T(8,128)(2,1)S(1)} %copy-done.1, f32[8,8,128]{2,1,0:T(8,128)S(1)} %get-tuple-element.7.refs_0_), custom_call_target="tpu_custom_call" | custom-call | flops 5000000000 | bytes 10000000 | tf_op jit(solution)/shard_map/products/pallas_call | solution.py:307
  18.7 0.2 collective-permute-done
  18.9 0.0 copy-start
  18.9 3.7 %collective-permute-start.1 = (bf16[2,104,128]{2,1,0:T(8,128)(2,1)S(1)}, bf16[2,104,128]{2,1,0:T(8,128)(2,1)S(1)}, u32[]{:S(2)}, u32[]{:S(2)}) collective-permute-start(bf16[2,104,128]{2,1,0:T(8,128)(2,1)S(1)} %pad_maximum_fusion), channel_id=1, source_target_pairs={{0,6},{1,7},{2,4},{3,5},{4,2},{5,3},{6,0},{7,1},{8,14},{9,15},{10,... | collective-permute-start | bytes 159752 | tf_op jit(solution)/shard_map/ppermute | solution.py:332
  22.6 0.1 collective-permute-start.2
  22.7 0.8 %collective-permute-start.3 = (bf16[2,104,128]{2,1,0:T(8,128)(2,1)S(1)}, bf16[2,104,128]{2,1,0:T(8,128)(2,1)S(1)}, u32[]{:S(2)}, u32[]{:S(2)}) collective-permute-start(bf16[2,104,128]{2,1,0:T(8,128)(2,1)S(1)} %pad_maximum_fusion.2), channel_id=1, source_target_pairs={{0,2},{1,3},{2,0},{3,1},{4,6},{5,7},{6,4},{7,5},{8,10},{9,11},{10,... | collective-permute-start | bytes 159752 | tf_op jit(solution)/shard_map/ppermute | solution.py:332
  23.5 0.4 %products.4.refs_0_ = bf16[1,104,128]{2,1,0:T(8,128)(2,1)S(1)} custom-call(s32[96,128]{1,0:T(8,128)S(1)} %broadcast_in_dim.4.cols_ref, s32[96,128]{1,0:T(8,128)S(1)} %broadcast_in_dim.5.rows_ref, bf16[4,34,24,128]{3,2,1,0:T(8,128)(2,1)S(1)} %bitcast.4, bf16[3,96,128,128]{3,2,1,0:T(8,128)(2,1)S(1)} %copy-done.1, f32[8,8,128]{2,1,0:T(8,128)S(1)} %get-tuple-element.7.refs_0_), custom_call_target="tpu_custom_call" | custom-call | flops 5000000000 | bytes 10000000 | tf_op jit(solution)/shard_map/products/pallas_call | solution.py:307
  24.0 1.1 %collective-permute-done.1.refs_2_ = bf16[2,104,128]{2,1,0:T(8,128)(2,1)S(1)} collective-permute-done((bf16[2,104,128]{2,1,0:T(8,128)(2,1)S(1)}, bf16[2,104,128]{2,1,0:T(8,128)(2,1)S(1)}, u32[]{:S(2)}, u32[]{:S(2)}) %collective-permute-start.1) | collective-permute-done | bytes 53280 | tf_op jit(solution)/shard_map/ppermute | solution.py:332
  25.0 2.9 %collective-permute-done.2.refs_3_ = bf16[2,104,128]{2,1,0:T(8,128)(2,1)S(1)} collective-permute-done((bf16[2,104,128]{2,1,0:T(8,128)(2,1)S(1)}, bf16[2,104,128]{2,1,0:T(8,128)(2,1)S(1)}, u32[]{:S(2)}, u32[]{:S(2)}) %collective-permute-start.2) | collective-permute-done | bytes 53280 | tf_op jit(solution)/shard_map/ppermute | solution.py:332
  27.9 0.1 collective-permute-done.3.refs_4_
  28.0 1.1 %merge.1 = (f32[8,4096]{1,0:T(8,128)S(1)}, f32[32,4,128]{2,1,0:T(4,128)S(1)}) custom-call(bf16[40,4096]{1,0:T(8,128)(2,1)S(1)} %copy-done, bf16[1,104,128]{2,1,0:T(8,128)(2,1)S(1)} %products.4.refs_0_, bf16[1,104,128]{2,1,0:T(8,128)(2,1)S(1)} %get-tuple-element.14.refs_1_, bf16[2,104,128]{2,1,0:T(8,128)(2,1)S(1)} %collective-permute-done.1.refs_2_, ...), custom_call_target="tpu_custom_call" | custom-call | tf_op jit(solution)/shard_map/merge/pallas_call | solution.py:333
  29.1 10.7 %all_to_all.5.packets_ref = f32[32,4,128]{2,1,0:T(4,128)S(1)} all-to-all(f32[32,4,128]{2,1,0:T(4,128)S(1)} %get-tuple-element.9), channel_id=1, replica_groups=mesh['row'=4,'col'=8] {'row','col'}, dimensions={0} | all-to-all | bytes 131072 | tf_op jit(solution)/shard_map/all_to_all | solution.py:345
  39.8 1.6 %finish.1 = (f32[8,4096]{1,0:T(8,128)}, f32[8,40]{1,0:T(8,128)}, f32[8,8]{1,0:T(8,128)}) custom-call(f32[32,4,128]{2,1,0:T(4,128)S(1)} %all_to_all.5.packets_ref, f32[8,4096]{1,0:T(8,128)S(1)} %get-tuple-element.10.applied_ref, bf16[40,4096]{1,0:T(8,128)(2,1)S(1)} %copy-done), custom_call_target="tpu_custom_call" | custom-call | tf_op jit(solution)/shard_map/finish/pallas_call | solution.py:346
  (7 shorter events, 0.1 us)
Async XLA Ops:
  0.6 15.3 %copy-start.2 = (s32[96]{0:T(128)S(1)}, s32[96]{0:T(128)}, u32[]{:S(2)}) copy-start(s32[96]{0:T(128)} %param.8) | copy-start | bytes 1156
  0.6 15.4 %copy-start.3 = (s32[96]{0:T(128)S(1)}, s32[96]{0:T(128)}, u32[]{:S(2)}) copy-start(s32[96]{0:T(128)} %param.9) | copy-start | bytes 1156
  0.7 15.5 %copy-start.1 = (bf16[3,96,128,128]{3,2,1,0:T(8,128)(2,1)S(1)}, bf16[3,96,128,128]{3,2,1,0:T(8,128)(2,1)}, u32[]{:S(2)}) copy-start(bf16[3,96,128,128]{3,2,1,0:T(8,128)(2,1)} %tiles_ref.5) | copy-start | bytes 28311556
  17.6 1.3 %collective-permute-start = (bf16[4,104,128]{2,1,0:T(8,128)(2,1)S(1)}, bf16[4,104,128]{2,1,0:T(8,128)(2,1)S(1)}, u32[]{:S(2)}, u32[]{:S(2)}) collective-permute-start(bf16[4,104,128]{2,1,0:T(8,128)(2,1)S(1)} %get-tuple-element.8), channel_id=1, source_target_pairs={{0,1},{1,0},{2,3},{3,2},{4,5},{5,4},{6,7},{7,6},{8,9},{9,8},{10,11... | collective-permute-start | bytes 319496 | tf_op jit(solution)/shard_map/ppermute | solution.py:325
  18.9 9.1 %copy-start = (bf16[40,4096]{1,0:T(8,128)(2,1)S(1)}, bf16[40,4096]{1,0:T(8,128)(2,1)}, u32[]{:S(2)}) copy-start(bf16[40,4096]{1,0:T(8,128)(2,1)} %basis_ref.5) | copy-start | bytes 983044
  18.9 6.1 %collective-permute-start.1 = (bf16[2,104,128]{2,1,0:T(8,128)(2,1)S(1)}, bf16[2,104,128]{2,1,0:T(8,128)(2,1)S(1)}, u32[]{:S(2)}, u32[]{:S(2)}) collective-permute-start(bf16[2,104,128]{2,1,0:T(8,128)(2,1)S(1)} %pad_maximum_fusion), channel_id=1, source_target_pairs={{0,6},{1,7},{2,4},{3,5},{4,2},{5,3},{6,0},{7,1},{8,14},{9,15},{10,... | collective-permute-start | bytes 159752 | tf_op jit(solution)/shard_map/ppermute | solution.py:332
  22.6 5.3 %collective-permute-start.2 = (bf16[2,104,128]{2,1,0:T(8,128)(2,1)S(1)}, bf16[2,104,128]{2,1,0:T(8,128)(2,1)S(1)}, u32[]{:S(2)}, u32[]{:S(2)}) collective-permute-start(bf16[2,104,128]{2,1,0:T(8,128)(2,1)S(1)} %pad_maximum_fusion.1), channel_id=1, source_target_pairs={{0,4},{1,5},{2,6},{3,7},{4,0},{5,1},{6,2},{7,3},{8,12},{9,13},{10,... | collective-permute-start | bytes 159752 | tf_op jit(solution)/shard_map/ppermute | solution.py:332
  22.7 5.3 %collective-permute-start.3 = (bf16[2,104,128]{2,1,0:T(8,128)(2,1)S(1)}, bf16[2,104,128]{2,1,0:T(8,128)(2,1)S(1)}, u32[]{:S(2)}, u32[]{:S(2)}) collective-permute-start(bf16[2,104,128]{2,1,0:T(8,128)(2,1)S(1)} %pad_maximum_fusion.2), channel_id=1, source_target_pairs={{0,2},{1,3},{2,0},{3,1},{4,6},{5,7},{6,4},{7,5},{8,10},{9,11},{10,... | collective-permute-start | bytes 159752 | tf_op jit(solution)/shard_map/ppermute | solution.py:332
where the time goes:
time: 41.6 us; the launch traced here: 41.4 us
  blocking collectives  24.3 us (58%)
  Pallas kernels  7.33 us (18%)
  starting transfers between devices  4.56 us (11%)
  waiting for transfers between devices  4.22 us (10%)
  between operations  0.73 us (2%)
    all_gather x1, blocking collectives, shards(): gathered = lax.all_gather(series, 'row', axis=0)  13.7 us
    all_to_all x1, blocking collectives, shards(): packets = lax.all_to_all(packet, ('row', 'col'), 0, 0, tiled=True)  10.7 us
    ppermute x3, starting transfers between devices, shards(): blocks.append(lax.ppermute(pair, 'col', moves))  4.56 us
    ppermute x3, waiting for transfers between devices, shards(): blocks.append(lax.ppermute(pair, 'col', moves))  4.07 us
    pallas_call x3, Pallas kernels, products(): pl.pallas_call(functools.partial(tile_kernel, sizes, core, distances, fir...  3 us
    pallas_call x1, Pallas kernels, shards(): pl.pallas_call(functools.partial(finish_kernel, (krylov, vectors, share,...  1.64 us
    pallas_call x1, Pallas kernels, shards(): pl.pallas_call(functools.partial(series_kernel, region, tile, extra), out...  1.62 us
    pallas_call x1, Pallas kernels, shards(): pl.pallas_call(functools.partial(merge_kernel, (region, krylov, cap, vect...  1.07 us
  transfers between devices with their start and end apart: 4, of which 4 were waited for; matrix products, arithmetic and copies ran while one was open for 0% of the time, Pallas kernels for 4%

commit v1 on v0

--- a/solution.py
+++ b/solution.py
@@ -25,7 +25,7 @@
     return high, middle, rest - middle
 
 
-def series_kernel(region, tile, extra, basis_ref, expand_ref, out_ref, scratch, here, small, sems):
+def series_kernel(region, tile, basis_ref, expand_ref, out_ref, scratch, here, small, sems):
     rows, krylov = expand_ref.shape
     copies = [
         pltpu.make_async_copy(basis_ref, here, sems.at[0]),
@@ -44,22 +44,31 @@
         out_ref[t] = series[:, t * tile : (t + 1) * tile]
     local = contract_lanes(basis, basis)
     high = local.astype(BF16).astype(F32)
-    scratch[:krylov, :krylov] = high
-    scratch[:krylov, HALF : HALF + krylov] = local - high
-    for e in range(extra):
-        out_ref[region + e] = scratch[e * rows : (e + 1) * rows, :].astype(BF16)
+    low = local - high
+    rest = krylov - rows
+    corner = 2 * krylov
+    scratch[:, :krylov] = high[:rows]
+    scratch[:, krylov:corner] = low[:rows]
+    scratch[:rest, corner : corner + rest] = high[rows:, rows:]
+    scratch[:rest, corner + rest : corner + 2 * rest] = low[rows:, rows:]
+    out_ref[region] = scratch[...].astype(BF16)
 
 
 def share_correlation(sizes, gathered_ref, scratch, slices):
-    row_count, region, extra, krylov, _, _, share = sizes
-    rows, tile = gathered_ref.shape[2:]
-    total = jnp.zeros((extra * rows, tile), F32)
-    for r in range(row_count):
-        total += jnp.concatenate(
-            [gathered_ref[r, region + e].astype(F32) for e in range(extra)], axis=0
-        )
+    row_count, region, krylov, _, _, share = sizes
+    rows, _ = gathered_ref.shape[2:]
+    rest = krylov - rows
+    corner = 2 * krylov
+    total = gathered_ref[0, region].astype(F32)
+    for r in range(1, row_count):
+        total += gathered_ref[r, region].astype(F32)
+    top = total[:, :krylov] + total[:, krylov:corner]
+    square = (total[:, corner : corner + rest] + total[:, corner + rest : corner + 2 * rest])[:rest]
     scratch[...] = jnp.zeros_like(scratch)
-    merged = total[:krylov, :krylov] + total[:krylov, HALF : HALF + krylov]
+    scratch[:rows, :krylov] = top
+    scratch[rows:krylov, :rows] = top.T[rows:krylov]
+    scratch[rows:krylov, rows:krylov] = square
+    merged = scratch[:krylov, :krylov]
     high = merged.astype(BF16).astype(F32)
     scratch[:krylov, :krylov] = high
     scratch[:krylov, HALF : HALF + krylov] = merged - high
@@ -69,19 +78,28 @@
             slices[c, :share, :] = scratch[c * share : (c + 1) * share, :]
 
 
-def tile_kernel(sizes, core, distances, first, cols_ref, rows_ref, gathered_ref, tiles_ref, *refs):
-    _, region, _, _, cap, vectors, _ = sizes
+def placed(piece, code, place):
+    onehot = jnp.where(place == code, 1.0, 0.0).astype(BF16)
+    return jnp.dot(onehot[:, : piece.shape[0]], piece, preferred_element_type=F32)
+
+
+def tile_kernel(sizes, core, distances, kind, cols_ref, rows_ref, gathered_ref, tiles_ref, *refs):
+    _, region, _, cap, vectors, _ = sizes
     tile = tiles_ref.shape[2]
+    span = (cap + 1) * vectors
     position = lax.axis_index("col")
-    if first:
+    if kind == "first":
         out_ref, slices, scratch = refs
         share_correlation(sizes, gathered_ref, scratch, slices)
+    elif kind == "own":
+        slices, partner_ref, total_ref, small_ref, out_ref = refs
     else:
         slices, out_ref = refs
     lane = lax.broadcasted_iota(jnp.int32, (8, tile), 1)
     sublane = lax.broadcasted_iota(jnp.int32, (8, tile), 0)
-    slot = lane // vectors
-    inner = lane - slot * vectors
+    index = lax.rem(lane + core * (tile - span), tile)
+    slot = index // vectors
+    inner = index - slot * vectors
 
     def column(t):
         c = cols_ref[pl.ds(t, 1), :1][0, 0]
@@ -131,23 +149,35 @@
 
     for place, distance in enumerate(distances):
         block(distance, place)
-
-
-def merge_kernel(sizes, basis_ref, *refs):
+    if kind == "own":
+        place = lax.broadcasted_iota(jnp.int32, (region * vectors, tile), 0).astype(F32)
+        total = jnp.zeros((region * vectors, tile), F32)
+        small = jnp.zeros((vectors, tile), F32)
+        for piece, shift in ((out_ref[0], 0), (partner_ref[partner_ref.shape[0] - 1], tile - span)):
+            last = piece[cap * vectors :].astype(F32)
+            small += last
+            code = pltpu.roll(last, shift, 1) if shift else last
+            total += placed(piece, code[7:8, :], place)
+        total_ref[...] = total
+        small_ref[...] = small
+
+
+def merge_kernel(sizes, basis_ref, total_ref, small_ref, *refs):
     region, krylov, cap, vectors, each = sizes
     blocks, (applied_ref, packet_ref, scratch) = refs[:-3], refs[-3:]
     tile = applied_ref.shape[1] // region
-    total = jnp.zeros((region * vectors, tile), F32)
-    small = jnp.zeros((vectors, tile), F32)
-    place = lax.broadcasted_iota(jnp.int32, (region * vectors, tile), 0).astype(F32)
+    total = total_ref[...]
+    small = small_ref[...]
+    place = lax.broadcasted_iota(jnp.int32, (region * vectors, 2 * tile), 0).astype(F32)
     span = (cap + 1) * vectors
+    row_lane = lax.broadcasted_iota(jnp.int32, (1, tile), 1)
     for ref in blocks:
-        for part in range(ref.shape[0]):
-            piece = ref[part]
-            last = piece[cap * vectors :].astype(F32)
-            small += last
-            onehot = jnp.where(place == last[7:8, :], 1.0, 0.0).astype(BF16)
-            total += jnp.dot(onehot[:, :span], piece, preferred_element_type=F32)
+        piece = ref[...]
+        near = piece[cap * vectors : span].astype(F32)
+        far = piece[span + cap * vectors :].astype(F32)
+        small += near + far
+        code = jnp.where(row_lane < span, near[7:8, :], far[7:8, :])
+        total += placed(piece, jnp.concatenate([code, far[7:8, :]], axis=1), place)
     for t in range(region):
         applied_ref[:, t * tile : (t + 1) * tile] = total[t * vectors : (t + 1) * vectors]
     applied = applied_ref[...]
@@ -268,23 +298,22 @@
     devices = row_count * col_count
     entries = length * devices
     cap = tiles.shape[1] // col_count
-    extra = -(-krylov // rows)
     share = -(-krylov // col_count)
     each = -(-share // row_count)
     span = (cap + 1) * vectors
     assert krylov + vectors < HALF and share < 8 and region * vectors <= 256
     assert each * -(-krylov // (HALF - krylov - vectors)) <= vectors and cap % 2 == 0
+    assert rows < krylov <= 2 * rows and 4 * krylov - 2 * rows <= tile
     vmem = pl.BlockSpec(memory_space=pltpu.VMEM)
-    smem = pl.BlockSpec(memory_space=pltpu.SMEM)
     hbm = pl.BlockSpec(memory_space=pltpu.HBM)
 
     series = pl.pallas_call(
-        functools.partial(series_kernel, region, tile, extra),
-        out_shape=jax.ShapeDtypeStruct((region + extra, rows, tile), BF16),
+        functools.partial(series_kernel, region, tile),
+        out_shape=jax.ShapeDtypeStruct((region + 1, rows, tile), BF16),
         in_specs=[hbm, hbm],
         out_specs=vmem,
         scratch_shapes=[
-            pltpu.VMEM((extra * rows, tile), F32),
+            pltpu.VMEM((rows, tile), F32),
             pltpu.VMEM(basis.shape, BF16),
             pltpu.VMEM((rows, krylov), F32),
             pltpu.SemaphoreType.DMA((2,)),
@@ -292,43 +321,50 @@
         cost_estimate=pl.CostEstimate(flops=10**10, bytes_accessed=10**7, transcendentals=0),
         compiler_params=pltpu.CompilerParams(vmem_limit_bytes=4 << 20),
         name="series",
-    )(pltpu.with_memory_space_constraint(basis, pltpu.HBM), pltpu.with_memory_space_constraint(expand.reshape(rows, krylov), pltpu.HBM))
+    )(
+        pltpu.with_memory_space_constraint(basis, pltpu.HBM),
+        pltpu.with_memory_space_constraint(expand.reshape(rows, krylov), pltpu.HBM),
+    )
     gathered = lax.all_gather(series, "row", axis=0)
     half = col_count // 2
-    sizes = (row_count, region, extra, krylov, cap, vectors, share)
-    table = jax.ShapeDtypeStruct((col_count, 8, tile), F32)
-
+    sizes = (row_count, region, krylov, cap, vectors, share)
     wide_cols = jnp.broadcast_to(tile_cols[:, None], (tile_cols.shape[0], tile))
-    wide_rows = jnp.broadcast_to(tile_rows[:, None], (tile_cols.shape[0], tile))
-
-    def products(core, distances, *slices):
-        first = not slices
-        outgoing = jax.ShapeDtypeStruct((len(distances), span, tile), BF16)
+    wide_rows = jnp.broadcast_to(tile_rows[:, None], (tile_rows.shape[0], tile))
+
+    def products(kind, core, distances, *rest):
+        outgoing = (len(distances), span, tile)
+        shapes = {
+            "first": ((outgoing, BF16), ((col_count, 8, tile), F32)),
+            "mine": ((outgoing, BF16),),
+            "own": (((region * vectors, tile), F32), ((vectors, tile), F32)),
+        }[kind]
+        scratch = {
+            "first": [pltpu.VMEM((max(krylov, share * col_count), tile), F32)],
+            "mine": [],
+            "own": [pltpu.VMEM(outgoing, BF16)],
+        }[kind]
         return pl.pallas_call(
-            functools.partial(tile_kernel, sizes, core, distances, first),
-            out_shape=(outgoing, table) if first else outgoing,
-            in_specs=[vmem, vmem, vmem, vmem] + [vmem] * len(slices),
-            out_specs=(vmem, vmem) if first else vmem,
-            scratch_shapes=[
-                pltpu.VMEM((max(extra * rows, share * col_count), tile), F32)
-            ] * first,
+            functools.partial(tile_kernel, sizes, core, distances, kind),
+            out_shape=tuple(jax.ShapeDtypeStruct(*shape) for shape in shapes),
+            in_specs=[vmem] * (4 + len(rest)),
+            out_specs=(vmem,) * len(shapes),
+            scratch_shapes=scratch,
             cost_estimate=pl.CostEstimate(
                 flops=5 * 10**9, bytes_accessed=10**7, transcendentals=0
             ),
             compiler_params=pltpu.CompilerParams(vmem_limit_bytes=16 << 20),
             name="products",
-        )(wide_cols, wide_rows, gathered, tiles, *slices)
+        )(wide_cols, wide_rows, gathered, tiles, *rest)
 
     apart = tuple(range(half - 1, 0, -1))
     swap = [(i, i ^ 1) for i in range(col_count)]
-    other, slices = products(1, apart + (0,))
+    other, slices = products("first", 1, apart + (0,))
     partner = lax.ppermute(other, "col", swap)
-    mine = products(0, apart, slices)
-    own = products(0, (0,), slices)
-    blocks = [own, partner[half - 1 :]]
+    (mine,) = products("mine", 0, apart, slices)
+    blocks = list(products("own", 0, (0,), slices, partner))
     for place, distance in enumerate(apart):
         moves = [(i, i ^ (2 * distance)) for i in range(col_count)]
-        pair = jnp.stack([mine[place], partner[place]])
+        pair = jnp.concatenate([mine[place], partner[place]], axis=0)
         blocks.append(lax.ppermute(pair, "col", moves))
     applied, packet = pl.pallas_call(
         functools.partial(merge_kernel, (region, krylov, cap, vectors, each)),

time: 41.6 us -> 40.9 us (0.983)
  blocking collectives: 24.3 us -> 23.8 us
    all_gather x1, blocking collectives: 13.7 us -> 13.2 us  [shards(): gathered = lax.all_gather(series, 'row', axis=0)]
where the time goes in v1:
time: 40.9 us; the launch traced here: 40.7 us
  blocking collectives  23.8 us (58%)
  Pallas kernels  7.43 us (18%)
  starting transfers between devices  4.44 us (11%)
  waiting for transfers between devices  4.1 us (10%)
  between operations  0.72 us (2%)
    all_gather x1, blocking collectives, shards(): gathered = lax.all_gather(series, 'row', axis=0)  13.2 us
    all_to_all x1, blocking collectives, shards(): packets = lax.all_to_all(packet, ('row', 'col'), 0, 0, tiled=True)  10.7 us
    ppermute x3, starting transfers between devices, shards(): blocks.append(lax.ppermute(pair, 'col', moves))  4.44 us
    ppermute x3, waiting for transfers between devices, shards(): blocks.append(lax.ppermute(pair, 'col', moves))  3.94 us
    pallas_call x3, Pallas kernels, products(): pl.pallas_call(functools.partial(tile_kernel, sizes, core, distances, kin...  3.2 us
    pallas_call x1, Pallas kernels, shards(): pl.pallas_call(functools.partial(finish_kernel, (krylov, vectors, share,...  1.64 us
    pallas_call x1, Pallas kernels, shards(): pl.pallas_call(functools.partial(series_kernel, region, tile), out_shape=...  1.62 us
    pallas_call x1, Pallas kernels, shards(): pl.pallas_call(functools.partial(merge_kernel, (region, krylov, cap, vect...  0.97 us
  transfers between devices with their start and end apart: 4, of which 4 were waited for; matrix products, arithmetic and copies ran while one was open for 0% of the time, Pallas kernels for 4%

profile of v1, /device:TPU:0, one launch (start us, length us, event | category | flops | bytes accessed | tf_op | source)
XLA Modules:
  0.0 40.7 jit_solution(2212141287660205251)
XLA Ops:
  0.6 0.0 copy-start.2
  0.6 0.0 copy-start.3
  0.7 0.0 copy-start.1
  0.7 1.6 %series.1 = bf16[33,24,128]{2,1,0:T(8,128)(2,1)S(1)} custom-call(bf16[40,4096]{1,0:T(8,128)(2,1)} %basis_ref.5, f32[24,40]{1,0:T(8,128)} %bitcast.17), custom_call_target="tpu_custom_call" | custom-call | flops 10000000000 | bytes 10000000 | tf_op jit(solution)/shard_map/series/pallas_call | solution.py:310
  2.3 13.2 %all-gather = bf16[132,24,128]{2,1,0:T(8,128)(2,1)S(1)} all-gather(bf16[33,24,128]{2,1,0:T(8,128)(2,1)S(1)} %series.1), channel_id=2, replica_groups=mesh['row'=4,'col'=8] {'row'}, dimensions={0}, use_global_device_ids=true | all-gather | bytes 1013760 | tf_op jit(solution)/shard_map/all_gather | solution.py:328
  15.4 0.0 copy-done.2
  15.5 0.1 broadcast_in_dim.5.rows_ref
  15.5 0.0 copy-done.3
  15.5 0.1 broadcast_in_dim.4.cols_ref
  15.6 0.0 copy-done.1
  15.6 1.4 %products.3 = (bf16[4,104,128]{2,1,0:T(8,128)(2,1)S(1)}, f32[8,8,128]{2,1,0:T(8,128)S(1)}) custom-call(s32[96,128]{1,0:T(8,128)S(1)} %broadcast_in_dim.4.cols_ref, s32[96,128]{1,0:T(8,128)S(1)} %broadcast_in_dim.5.rows_ref, bf16[4,33,24,128]{3,2,1,0:T(8,128)(2,1)S(1)} %bitcast.14, bf16[3,96,128,128]{3,2,1,0:T(8,128)(2,1)S(1)} %copy-done.1), custom_call_target="tpu_custom_call" | custom-call | flops 5000000000 | bytes 10000000 | tf_op jit(solution)/shard_map/products/pallas_call | solution.py:346
  17.1 0.0 collective-permute-start
  17.1 1.1 %products.5 = bf16[3,104,128]{2,1,0:T(8,128)(2,1)S(1)} custom-call(s32[96,128]{1,0:T(8,128)S(1)} %broadcast_in_dim.4.cols_ref, s32[96,128]{1,0:T(8,128)S(1)} %broadcast_in_dim.5.rows_ref, bf16[4,33,24,128]{3,2,1,0:T(8,128)(2,1)S(1)} %bitcast.15, bf16[3,96,128,128]{3,2,1,0:T(8,128)(2,1)S(1)} %copy-done.1, f32[8,8,128]{2,1,0:T(8,128)S(1)} %get-tuple-element.9.refs_0_), custom_call_target="tpu_custom_call" | custom-call | flops 5000000000 | bytes 10000000 | tf_op jit(solution)/shard_map/products/pallas_call | solution.py:346
  18.2 0.2 collective-permute-done.refs_1_
  18.4 3.7 %collective-permute-start.1 = (bf16[208,128]{1,0:T(8,128)(2,1)S(1)}, bf16[208,128]{1,0:T(8,128)(2,1)S(1)}, u32[]{:S(2)}, u32[]{:S(2)}) collective-permute-start(bf16[208,128]{1,0:T(8,128)(2,1)S(1)} %pad_maximum_fusion), channel_id=1, source_target_pairs={{0,6},{1,7},{2,4},{3,5},{4,2},{5,3},{6,0},{7,1},{8,14},{9,15},{10,... | collective-permute-start | bytes 159752 | tf_op jit(solution)/shard_map/ppermute | solution.py:368
  22.1 0.0 collective-permute-start.2
  22.1 0.8 %collective-permute-start.3 = (bf16[208,128]{1,0:T(8,128)(2,1)S(1)}, bf16[208,128]{1,0:T(8,128)(2,1)S(1)}, u32[]{:S(2)}, u32[]{:S(2)}) collective-permute-start(bf16[208,128]{1,0:T(8,128)(2,1)S(1)} %pad_maximum_fusion.2), channel_id=1, source_target_pairs={{0,2},{1,3},{2,0},{3,1},{4,6},{5,7},{6,4},{7,5},{8,10},{9,11},{10,... | collective-permute-start | bytes 159752 | tf_op jit(solution)/shard_map/ppermute | solution.py:368
  22.9 0.6 %products.4 = (f32[256,128]{1,0:T(8,128)S(1)}, f32[8,128]{1,0:T(8,128)S(1)}) custom-call(s32[96,128]{1,0:T(8,128)S(1)} %broadcast_in_dim.4.cols_ref, s32[96,128]{1,0:T(8,128)S(1)} %broadcast_in_dim.5.rows_ref, bf16[4,33,24,128]{3,2,1,0:T(8,128)(2,1)S(1)} %bitcast.16, bf16[3,96,128,128]{3,2,1,0:T(8,128)(2,1)S(1)} %copy-done.1, ...), custom_call_target="tpu_custom_call" | custom-call | flops 5000000000 | bytes 10000000 | tf_op jit(solution)/shard_map/products/pallas_call | solution.py:346
  23.5 1.0 %collective-permute-done.1.refs_0_ = bf16[208,128]{1,0:T(8,128)(2,1)S(1)} collective-permute-done((bf16[208,128]{1,0:T(8,128)(2,1)S(1)}, bf16[208,128]{1,0:T(8,128)(2,1)S(1)}, u32[]{:S(2)}, u32[]{:S(2)}) %collective-permute-start.1) | collective-permute-done | bytes 53280 | tf_op jit(solution)/shard_map/ppermute | solution.py:368
  24.5 2.8 %collective-permute-done.2.refs_1_ = bf16[208,128]{1,0:T(8,128)(2,1)S(1)} collective-permute-done((bf16[208,128]{1,0:T(8,128)(2,1)S(1)}, bf16[208,128]{1,0:T(8,128)(2,1)S(1)}, u32[]{:S(2)}, u32[]{:S(2)}) %collective-permute-start.2) | collective-permute-done | bytes 53280 | tf_op jit(solution)/shard_map/ppermute | solution.py:368
  27.3 0.1 collective-permute-done.3.refs_2_
  27.4 1.0 %merge.1 = (f32[8,4096]{1,0:T(8,128)S(1)}, f32[32,4,128]{2,1,0:T(4,128)S(1)}) custom-call(bf16[40,4096]{1,0:T(8,128)(2,1)S(1)} %copy-done, f32[256,128]{1,0:T(8,128)S(1)} %get-tuple-element.11.total_ref, f32[8,128]{1,0:T(8,128)S(1)} %get-tuple-element.12.small_ref, bf16[208,128]{1,0:T(8,128)(2,1)S(1)} %collective-permute-done.1.refs_0_, ...), custom_call_target="tpu_custom_call" | custom-call | tf_op jit(solution)/shard_map/merge/pallas_call | solution.py:369
  28.4 10.7 %all_to_all.5.packets_ref = f32[32,4,128]{2,1,0:T(4,128)S(1)} all-to-all(f32[32,4,128]{2,1,0:T(4,128)S(1)} %get-tuple-element.13), channel_id=1, replica_groups=mesh['row'=4,'col'=8] {'row','col'}, dimensions={0} | all-to-all | bytes 131072 | tf_op jit(solution)/shard_map/all_to_all | solution.py:381
  39.1 1.6 %finish.1 = (f32[8,4096]{1,0:T(8,128)}, f32[8,40]{1,0:T(8,128)}, f32[8,8]{1,0:T(8,128)}) custom-call(f32[32,4,128]{2,1,0:T(4,128)S(1)} %all_to_all.5.packets_ref, f32[8,4096]{1,0:T(8,128)S(1)} %get-tuple-element.14.applied_ref, bf16[40,4096]{1,0:T(8,128)(2,1)S(1)} %copy-done), custom_call_target="tpu_custom_call" | custom-call | tf_op jit(solution)/shard_map/finish/pallas_call | solution.py:382
  (7 shorter events, 0.1 us)
Async XLA Ops:
  0.6 14.8 %copy-start.2 = (s32[96]{0:T(128)S(1)}, s32[96]{0:T(128)}, u32[]{:S(2)}) copy-start(s32[96]{0:T(128)} %param.8) | copy-start | bytes 1156
  0.6 14.9 %copy-start.3 = (s32[96]{0:T(128)S(1)}, s32[96]{0:T(128)}, u32[]{:S(2)}) copy-start(s32[96]{0:T(128)} %param.9) | copy-start | bytes 1156
  0.7 15.0 %copy-start.1 = (bf16[3,96,128,128]{3,2,1,0:T(8,128)(2,1)S(1)}, bf16[3,96,128,128]{3,2,1,0:T(8,128)(2,1)}, u32[]{:S(2)}) copy-start(bf16[3,96,128,128]{3,2,1,0:T(8,128)(2,1)} %tiles_ref.5) | copy-start | bytes 28311556
  17.1 1.3 %collective-permute-start = (bf16[4,104,128]{2,1,0:T(8,128)(2,1)S(1)}, bf16[4,104,128]{2,1,0:T(8,128)(2,1)S(1)}, u32[]{:S(2)}, u32[]{:S(2)}) collective-permute-start(bf16[4,104,128]{2,1,0:T(8,128)(2,1)S(1)} %get-tuple-element.10), channel_id=1, source_target_pairs={{0,1},{1,0},{2,3},{3,2},{4,5},{5,4},{6,7},{7,6},{8,9},{9,8},{10,11... | collective-permute-start | bytes 319496 | tf_op jit(solution)/shard_map/ppermute | solution.py:362
  18.4 9.1 %copy-start = (bf16[40,4096]{1,0:T(8,128)(2,1)S(1)}, bf16[40,4096]{1,0:T(8,128)(2,1)}, u32[]{:S(2)}) copy-start(bf16[40,4096]{1,0:T(8,128)(2,1)} %basis_ref.5) | copy-start | bytes 983044
  18.4 6.1 %collective-permute-start.1 = (bf16[208,128]{1,0:T(8,128)(2,1)S(1)}, bf16[208,128]{1,0:T(8,128)(2,1)S(1)}, u32[]{:S(2)}, u32[]{:S(2)}) collective-permute-start(bf16[208,128]{1,0:T(8,128)(2,1)S(1)} %pad_maximum_fusion), channel_id=1, source_target_pairs={{0,6},{1,7},{2,4},{3,5},{4,2},{5,3},{6,0},{7,1},{8,14},{9,15},{10,... | collective-permute-start | bytes 159752 | tf_op jit(solution)/shard_map/ppermute | solution.py:368
  22.1 5.3 %collective-permute-start.2 = (bf16[208,128]{1,0:T(8,128)(2,1)S(1)}, bf16[208,128]{1,0:T(8,128)(2,1)S(1)}, u32[]{:S(2)}, u32[]{:S(2)}) collective-permute-start(bf16[208,128]{1,0:T(8,128)(2,1)S(1)} %pad_maximum_fusion.1), channel_id=1, source_target_pairs={{0,4},{1,5},{2,6},{3,7},{4,0},{5,1},{6,2},{7,3},{8,12},{9,13},{10,... | collective-permute-start | bytes 159752 | tf_op jit(solution)/shard_map/ppermute | solution.py:368
  22.1 5.3 %collective-permute-start.3 = (bf16[208,128]{1,0:T(8,128)(2,1)S(1)}, bf16[208,128]{1,0:T(8,128)(2,1)S(1)}, u32[]{:S(2)}, u32[]{:S(2)}) collective-permute-start(bf16[208,128]{1,0:T(8,128)(2,1)S(1)} %pad_maximum_fusion.2), channel_id=1, source_target_pairs={{0,2},{1,3},{2,0},{3,1},{4,6},{5,7},{6,4},{7,5},{8,10},{9,11},{10,... | collective-permute-start | bytes 159752 | tf_op jit(solution)/shard_map/ppermute | solution.py:368

commit v2 on v1

--- a/solution.py
+++ b/solution.py
@@ -25,21 +25,27 @@
     return high, middle, rest - middle
 
 
-def series_kernel(region, tile, basis_ref, expand_ref, out_ref, scratch, here, small, sems):
+def series_kernel(
+    region, tile, basis_ref, expand_ref, cols_ref, rows_ref, out_ref, *refs
+):
+    tables, (scratch, here, small, lists, sems) = refs[:2], refs[2:]
     rows, krylov = expand_ref.shape
-    copies = [
-        pltpu.make_async_copy(basis_ref, here, sems.at[0]),
-        pltpu.make_async_copy(expand_ref, small, sems.at[1]),
-    ]
+    groups = basis_ref.shape[0] // 8
+    copies = [pltpu.make_async_copy(expand_ref, small, sems.at[groups])]
+    copies.append(pltpu.make_async_copy(cols_ref, lists.at[0], sems.at[groups + 1]))
+    copies.append(pltpu.make_async_copy(rows_ref, lists.at[1], sems.at[groups + 2]))
+    for g in range(groups):
+        part = pl.ds(8 * g, 8)
+        copies.append(pltpu.make_async_copy(basis_ref.at[part], here.at[part], sems.at[g]))
     for copy in copies:
         copy.start()
     scratch[...] = jnp.zeros_like(scratch)
     for copy in copies:
         copy.wait()
     basis = here[...]
-    parts = jnp.concatenate(split3(small[...]), axis=0).astype(BF16)
+    parts = jnp.concatenate(split3(small[...])[:2], axis=0).astype(BF16)
     wide = jnp.dot(parts, basis, preferred_element_type=F32)
-    series = (wide[:rows] + wide[rows : 2 * rows] + wide[2 * rows :]).astype(BF16)
+    series = (wide[:rows] + wide[rows:]).astype(BF16)
     for t in range(region):
         out_ref[t] = series[:, t * tile : (t + 1) * tile]
     local = contract_lanes(basis, basis)
@@ -52,6 +58,9 @@
     scratch[:rest, corner : corner + rest] = high[rows:, rows:]
     scratch[:rest, corner + rest : corner + 2 * rest] = low[rows:, rows:]
     out_ref[region] = scratch[...].astype(BF16)
+    for k, table in enumerate(tables):
+        spread = jnp.broadcast_to(lists[k].astype(F32), (tile, lists.shape[2]))
+        table[...] = spread.T.astype(jnp.int32)
 
 
 def share_correlation(sizes, gathered_ref, scratch, slices):
@@ -83,23 +92,21 @@
     return jnp.dot(onehot[:, : piece.shape[0]], piece, preferred_element_type=F32)
 
 
-def tile_kernel(sizes, core, distances, kind, cols_ref, rows_ref, gathered_ref, tiles_ref, *refs):
+def tile_kernel(sizes, groups, first, cols_ref, rows_ref, gathered_ref, tiles_ref, *refs):
+    refs, turned = refs[:-1], refs[-1]
+    used = []
     _, region, _, cap, vectors, _ = sizes
     tile = tiles_ref.shape[2]
     span = (cap + 1) * vectors
     position = lax.axis_index("col")
-    if kind == "first":
-        out_ref, slices, scratch = refs
+    if first:
+        slices, scratch = refs[-2:]
+        out_refs = refs[:-2]
         share_correlation(sizes, gathered_ref, scratch, slices)
-    elif kind == "own":
-        slices, partner_ref, total_ref, small_ref, out_ref = refs
     else:
-        slices, out_ref = refs
+        slices, out_refs = refs[0], refs[1:]
     lane = lax.broadcasted_iota(jnp.int32, (8, tile), 1)
     sublane = lax.broadcasted_iota(jnp.int32, (8, tile), 0)
-    index = lax.rem(lane + core * (tile - span), tile)
-    slot = index // vectors
-    inner = index - slot * vectors
 
     def column(t):
         c = cols_ref[pl.ds(t, 1), :1][0, 0]
@@ -110,11 +117,20 @@
     def weights(m, t):
         return tiles_ref[m, pl.ds(t, 2)].reshape(2 * tile, tile)
 
+    def through(lhs, rhs):
+        slot = len(used)
+        used.append(slot)
+        turned[slot] = rhs.T
+        return jnp.dot(lhs, turned[slot], preferred_element_type=F32)
+
     def side(a, b):
         return jnp.concatenate([a, b], axis=1)
 
-    def block(distance, place):
+    def block(core, distance, out_ref, place):
         target = (position ^ (2 * distance)) ^ core
+        index = lax.rem(lane + core * (tile - span), tile)
+        slot = index // vectors
+        inner = index - slot * vectors
         base = target * cap
 
         def store(p, out):
@@ -128,7 +144,8 @@
             lhs = jnp.concatenate([side(x0[0], x0[1]), side(x1[0], x1[1])], axis=0)
             rhs = side(weights(0, t), weights(1, t))
             third = jnp.concatenate([x0[2], x1[2]], axis=0)
-            pairs.append((p, contract_lanes(lhs, rhs), third, weights(2, t)))
+            out = through(lhs, rhs)
+            pairs.append((p, out, third, weights(2, t)))
         while len(pairs) > 1:
             (p, out_p, x_p, w_p), (q, out_q, x_q, w_q) = pairs[:2]
             pairs = pairs[2:]
@@ -147,19 +164,25 @@
         last = jnp.where(sublane == 7, code.astype(F32), slices[target])
         out_ref[place, cap * vectors : (cap + 1) * vectors, :] = last.astype(BF16)
 
-    for place, distance in enumerate(distances):
-        block(distance, place)
-    if kind == "own":
-        place = lax.broadcasted_iota(jnp.int32, (region * vectors, tile), 0).astype(F32)
-        total = jnp.zeros((region * vectors, tile), F32)
-        small = jnp.zeros((vectors, tile), F32)
-        for piece, shift in ((out_ref[0], 0), (partner_ref[partner_ref.shape[0] - 1], tile - span)):
-            last = piece[cap * vectors :].astype(F32)
-            small += last
-            code = pltpu.roll(last, shift, 1) if shift else last
-            total += placed(piece, code[7:8, :], place)
-        total_ref[...] = total
-        small_ref[...] = small
+    for group, out_ref in zip(groups, out_refs):
+        for place, (core, distance) in enumerate(group):
+            block(core, distance, out_ref, place)
+
+
+def own_kernel(sizes, own_ref, partner_ref, total_ref, small_ref):
+    _, _, _, cap, vectors, _ = sizes
+    tile = total_ref.shape[1]
+    span = (cap + 1) * vectors
+    place = lax.broadcasted_iota(jnp.int32, total_ref.shape, 0).astype(F32)
+    total = jnp.zeros(total_ref.shape, F32)
+    small = jnp.zeros(small_ref.shape, F32)
+    for piece, shift in ((own_ref[0], 0), (partner_ref[0], tile - span)):
+        last = piece[cap * vectors :].astype(F32)
+        small += last
+        code = pltpu.roll(last, shift, 1) if shift else last
+        total += placed(piece, code[7:8, :], place)
+    total_ref[...] = total
+    small_ref[...] = small
 
 
 def merge_kernel(sizes, basis_ref, total_ref, small_ref, *refs):
@@ -224,7 +247,6 @@
 ):
     krylov, vectors, share, each, col_count, entries = sizes
     inverse_root = 1.0 / math.sqrt(entries)
-    highest = lax.Precision.HIGHEST
     devices, half, tile = packets_ref.shape
     folded = tree_sum([packets_ref[d] for d in range(devices)])
     total = jnp.concatenate([folded, pltpu.roll(folded, HALF, 1)], axis=0)
@@ -247,24 +269,29 @@
     correlation = scratch[:krylov, :krylov] * (1.0 / entries)
     first = total[:, :krylov] * inverse_root
     energy = total[:, krylov : krylov + vectors]
-    dot = functools.partial(jnp.dot, precision=highest, preferred_element_type=F32)
-    across = functools.partial(
-        lax.dot_general,
-        dimension_numbers=(((1,), (1,)), ((), ())),
-        precision=highest,
-        preferred_element_type=F32,
-    )
-    coefficients = first + (first - dot(first, correlation))
+    corr_high = correlation.astype(BF16)
+    corr_low = (correlation - corr_high.astype(F32)).astype(BF16)
+
+    def halves(value):
+        high = value.astype(BF16).astype(F32)
+        return high.astype(BF16), jnp.concatenate([high, value - high], axis=0).astype(BF16)
+
+    def times_correlation(value):
+        high, both = halves(value)
+        main = jnp.dot(both, corr_high, preferred_element_type=F32)
+        rest = jnp.dot(high, corr_low, preferred_element_type=F32)
+        return main[:vectors] + (main[vectors:] + rest)
+
+    coefficients = first + (first - times_correlation(first))
     coefficients_ref[...] = coefficients
-    parts = jnp.concatenate(split3(coefficients * inverse_root), axis=0).astype(BF16)
+    _, parts = halves(coefficients * inverse_root)
     wide = jnp.dot(parts, basis_ref[...], preferred_element_type=F32)
-    cleaned = applied_ref[...] - (
-        wide[:vectors] + (wide[vectors : 2 * vectors] + wide[2 * vectors :])
-    )
-    mixed = across(first, coefficients)
-    mixed_t = across(coefficients, first)
-    curved = across(dot(coefficients, correlation), coefficients)
-    gram = (energy - mixed - mixed_t + curved) * (1.0 / entries)
+    cleaned = applied_ref[...] - (wide[:vectors] + wide[vectors:])
+    coef_high, coef_both = halves(coefficients)
+    high, both = halves(times_correlation(coefficients) - 2.0 * first)
+    main = contract_lanes(both, coef_high)
+    rest = contract_lanes(high, coef_both[vectors:])
+    gram = (energy + main[:vectors] + (main[vectors:] + rest)) * (1.0 / entries)
     columns = [jnp.broadcast_to(gram[:, j : j + 1], (vectors, tile)) for j in range(vectors)]
     sublane = lax.broadcasted_iota(jnp.int32, (vectors, tile), 0)
     lane = lax.broadcasted_iota(jnp.int32, (vectors, tile), 1)
@@ -307,65 +334,87 @@
     vmem = pl.BlockSpec(memory_space=pltpu.VMEM)
     hbm = pl.BlockSpec(memory_space=pltpu.HBM)
 
-    series = pl.pallas_call(
+    count = tile_cols.shape[0]
+    index_table = jax.ShapeDtypeStruct((count, tile), jnp.int32)
+    series, wide_cols, wide_rows = pl.pallas_call(
         functools.partial(series_kernel, region, tile),
-        out_shape=jax.ShapeDtypeStruct((region + 1, rows, tile), BF16),
-        in_specs=[hbm, hbm],
-        out_specs=vmem,
+        out_shape=(
+            jax.ShapeDtypeStruct((region + 1, rows, tile), BF16),
+            index_table,
+            index_table,
+        ),
+        in_specs=[hbm] * 4,
+        out_specs=(vmem,) * 3,
         scratch_shapes=[
             pltpu.VMEM((rows, tile), F32),
             pltpu.VMEM(basis.shape, BF16),
             pltpu.VMEM((rows, krylov), F32),
-            pltpu.SemaphoreType.DMA((2,)),
+            pltpu.VMEM((2, 1, count), jnp.int32),
+            pltpu.SemaphoreType.DMA((krylov // 8 + 3,)),
         ],
         cost_estimate=pl.CostEstimate(flops=10**10, bytes_accessed=10**7, transcendentals=0),
         compiler_params=pltpu.CompilerParams(vmem_limit_bytes=4 << 20),
         name="series",
     )(
-        pltpu.with_memory_space_constraint(basis, pltpu.HBM),
-        pltpu.with_memory_space_constraint(expand.reshape(rows, krylov), pltpu.HBM),
+        *(
+            pltpu.with_memory_space_constraint(value, pltpu.HBM)
+            for value in (
+                basis,
+                expand.reshape(rows, krylov),
+                tile_cols.reshape(1, count),
+                tile_rows.reshape(1, count),
+            )
+        )
     )
     gathered = lax.all_gather(series, "row", axis=0)
     half = col_count // 2
     sizes = (row_count, region, krylov, cap, vectors, share)
-    wide_cols = jnp.broadcast_to(tile_cols[:, None], (tile_cols.shape[0], tile))
-    wide_rows = jnp.broadcast_to(tile_rows[:, None], (tile_rows.shape[0], tile))
-
-    def products(kind, core, distances, *rest):
-        outgoing = (len(distances), span, tile)
-        shapes = {
-            "first": ((outgoing, BF16), ((col_count, 8, tile), F32)),
-            "mine": ((outgoing, BF16),),
-            "own": (((region * vectors, tile), F32), ((vectors, tile), F32)),
-        }[kind]
-        scratch = {
-            "first": [pltpu.VMEM((max(krylov, share * col_count), tile), F32)],
-            "mine": [],
-            "own": [pltpu.VMEM(outgoing, BF16)],
-        }[kind]
+
+    def products(groups, *slices):
+        first = not slices
+        shapes = [((len(group), span, tile), BF16) for group in groups]
+        shapes += [((col_count, 8, tile), F32)] * first
         return pl.pallas_call(
-            functools.partial(tile_kernel, sizes, core, distances, kind),
+            functools.partial(tile_kernel, sizes, groups, first),
             out_shape=tuple(jax.ShapeDtypeStruct(*shape) for shape in shapes),
-            in_specs=[vmem] * (4 + len(rest)),
+            in_specs=[vmem] * (4 + len(slices)),
             out_specs=(vmem,) * len(shapes),
-            scratch_shapes=scratch,
+            scratch_shapes=[pltpu.VMEM((max(krylov, share * col_count), tile), F32)] * first
+            + [pltpu.VMEM((9 * max(1, sum(map(len, groups))), 2 * tile, 2 * tile), BF16)],
             cost_estimate=pl.CostEstimate(
                 flops=5 * 10**9, bytes_accessed=10**7, transcendentals=0
             ),
             compiler_params=pltpu.CompilerParams(vmem_limit_bytes=16 << 20),
             name="products",
-        )(wide_cols, wide_rows, gathered, tiles, *rest)
+        )(wide_cols, wide_rows, gathered, tiles, *slices)
 
     apart = tuple(range(half - 1, 0, -1))
+    far = apart
     swap = [(i, i ^ 1) for i in range(col_count)]
-    other, slices = products("first", 1, apart + (0,))
+    other, slices = products((tuple((1, d) for d in apart),))
     partner = lax.ppermute(other, "col", swap)
-    (mine,) = products("mine", 0, apart, slices)
-    blocks = list(products("own", 0, (0,), slices, partner))
-    for place, distance in enumerate(apart):
-        moves = [(i, i ^ (2 * distance)) for i in range(col_count)]
-        pair = jnp.concatenate([mine[place], partner[place]], axis=0)
-        blocks.append(lax.ppermute(pair, "col", moves))
+    (mine_far,) = products((tuple((0, d) for d in far),), slices)
+    other_here, own = products((((1, 0),), ((0, 0),)), slices)
+    partner_here = lax.ppermute(other_here, "col", swap)
+    blocks = list(
+        pl.pallas_call(
+            functools.partial(own_kernel, sizes),
+            out_shape=(
+                jax.ShapeDtypeStruct((region * vectors, tile), F32),
+                jax.ShapeDtypeStruct((vectors, tile), F32),
+            ),
+            in_specs=[vmem] * 2,
+            out_specs=(vmem,) * 2,
+            cost_estimate=pl.CostEstimate(flops=5 * 10**8, bytes_accessed=10**6, transcendentals=0),
+            compiler_params=pltpu.CompilerParams(vmem_limit_bytes=8 << 20),
+            name="own",
+        )(own, partner_here)
+    )
+    for distances, mine in ((far, mine_far),):
+        for place, distance in enumerate(distances):
+            moves = [(i, i ^ (2 * distance)) for i in range(col_count)]
+            pair = jnp.concatenate([mine[place], partner[apart.index(distance)]], axis=0)
+            blocks.append(lax.ppermute(pair, "col", moves))
     applied, packet = pl.pallas_call(
         functools.partial(merge_kernel, (region, krylov, cap, vectors, each)),
         out_shape=(

time: 40.9 us -> 40.9 us (level)
  Pallas kernels: 7.43 us -> 6.86 us
  starting transfers between devices: 4.44 us -> 4.96 us
    pallas_call x3 -> x4, Pallas kernels: 3.2 us -> 2.65 us  [the longest x3 2.43 us: products(): pl.pallas_call(functools.partial(tile_kernel, sizes, groups, first), out_...]
    ppermute x1, starting transfers between devices: 0.01 us -> 0.52 us  [shards(): partner = lax.ppermute(other, 'col', swap)]
    ppermute x3, waiting for transfers between devices: 3.94 us -> 4.35 us  [shards(): blocks.append(lax.ppermute(pair, 'col', moves))]
  transfers between devices with their start and end apart: 4 -> 5, of which waited for: 4 -> 3; matrix products, arithmetic and copies ran while one was open for 0% -> 0% of each run, Pallas kernels for 4% -> 3%
where the time goes in v2:
time: 40.9 us; the launch traced here: 40.8 us
  blocking collectives  23.8 us (58%)
  Pallas kernels  6.86 us (17%)
  starting transfers between devices  4.96 us (12%)
  waiting for transfers between devices  4.39 us (11%)
  between operations  0.69 us (2%)
    all_gather x1, blocking collectives, shards(): gathered = lax.all_gather(series, 'row', axis=0)  13.1 us
    all_to_all x1, blocking collectives, shards(): packets = lax.all_to_all(packet, ('row', 'col'), 0, 0, tiled=True)  10.7 us
    ppermute x3, starting transfers between devices, shards(): blocks.append(lax.ppermute(pair, 'col', moves))  4.44 us
    ppermute x3, waiting for transfers between devices, shards(): blocks.append(lax.ppermute(pair, 'col', moves))  4.35 us
    pallas_call x3, Pallas kernels, products(): pl.pallas_call(functools.partial(tile_kernel, sizes, groups, first), out_...  2.43 us
    pallas_call x1, Pallas kernels, shards(): pl.pallas_call(functools.partial(series_kernel, region, tile), out_shape=...  1.7 us
    pallas_call x1, Pallas kernels, shards(): pl.pallas_call(functools.partial(finish_kernel, (krylov, vectors, share,...  1.54 us
    pallas_call x1, Pallas kernels, shards(): pl.pallas_call(functools.partial(merge_kernel, (region, krylov, cap, vect...  0.96 us
  transfers between devices with their start and end apart: 5, of which 3 were waited for; matrix products, arithmetic and copies ran while one was open for 0% of the time, Pallas kernels for 3%

profile of v2, /device:TPU:0, one launch (start us, length us, event | category | flops | bytes accessed | tf_op | source)
XLA Modules:
  0.0 40.8 jit_solution(9271136919184389946)
XLA Ops:
  0.6 0.0 copy-start.1
  0.6 1.7 %series.1 = (bf16[33,24,128]{2,1,0:T(8,128)(2,1)S(1)}, s32[96,128]{1,0:T(8,128)S(1)}, s32[96,128]{1,0:T(8,128)S(1)}) custom-call(bf16[40,4096]{1,0:T(8,128)(2,1)} %basis_ref.5, f32[24,40]{1,0:T(8,128)} %bitcast.19, s32[1,96]{1,0:T(1,128)} %bitcast.20, s32[1,96]{1,0:T(1,128)} %bitcast.21), custom_call_target="tpu_custom_call" | custom-call | flops 10000000000 | bytes 10000000 | tf_op jit(solution)/shard_map/series/pallas_call | solution.py:339
  2.4 13.1 %all-gather = bf16[132,24,128]{2,1,0:T(8,128)(2,1)S(1)} all-gather(bf16[33,24,128]{2,1,0:T(8,128)(2,1)S(1)} %get-tuple-element.16), channel_id=2, replica_groups=mesh['row'=4,'col'=8] {'row'}, dimensions={0}, use_global_device_ids=true | all-gather | bytes 1013760 | tf_op jit(solution)/shard_map/all_gather | solution.py:369
  15.5 0.0 copy-done.1
  15.5 0.9 %products.3 = (bf16[3,104,128]{2,1,0:T(8,128)(2,1)S(1)}, f32[8,8,128]{2,1,0:T(8,128)S(1)}) custom-call(s32[96,128]{1,0:T(8,128)S(1)} %get-tuple-element.14.cols_ref, s32[96,128]{1,0:T(8,128)S(1)} %get-tuple-element.15.rows_ref, bf16[4,33,24,128]{3,2,1,0:T(8,128)(2,1)S(1)} %bitcast.16, bf16[3,96,128,128]{3,2,1,0:T(8,128)(2,1)S(1)} %copy-done.1), custom_call_target="tpu_custom_call" | custom-call | flops 5000000000 | bytes 10000000 | tf_op jit(solution)/shard_map/products/pallas_call | solution.py:377
  16.5 0.6 %products.4 = (bf16[1,104,128]{2,1,0:T(8,128)(2,1)S(1)}, bf16[1,104,128]{2,1,0:T(8,128)(2,1)S(1)}) custom-call(s32[96,128]{1,0:T(8,128)S(1)} %get-tuple-element.14.cols_ref, s32[96,128]{1,0:T(8,128)S(1)} %get-tuple-element.15.rows_ref, bf16[4,33,24,128]{3,2,1,0:T(8,128)(2,1)S(1)} %bitcast.17, bf16[3,96,128,128]{3,2,1,0:T(8,128)(2,1)S(1)} %copy-done.1, ...), custom_call_target="tpu_custom_call" | custom-call | flops 5000000000 | bytes 10000000 | tf_op jit(solution)/shard_map/products/pallas_call | solution.py:377
  17.1 0.0 collective-permute-start
  17.1 0.0 copy-start
  17.1 0.5 %collective-permute-start.1 = (bf16[3,104,128]{2,1,0:T(8,128)(2,1)S(1)}, bf16[3,104,128]{2,1,0:T(8,128)(2,1)S(1)}, u32[]{:S(2)}, u32[]{:S(2)}) collective-permute-start(bf16[3,104,128]{2,1,0:T(8,128)(2,1)S(1)} %get-tuple-element.22), channel_id=1, source_target_pairs={{0,1},{1,0},{2,3},{3,2},{4,5},{5,4},{6,7},{7,6},{8,9},{9,8},{10,11... | collective-permute-start | bytes 239624 | tf_op jit(solution)/shard_map/ppermute | solution.py:395
  17.6 0.9 %products.5 = bf16[3,104,128]{2,1,0:T(8,128)(2,1)S(1)} custom-call(s32[96,128]{1,0:T(8,128)S(1)} %get-tuple-element.14.cols_ref, s32[96,128]{1,0:T(8,128)S(1)} %get-tuple-element.15.rows_ref, bf16[4,33,24,128]{3,2,1,0:T(8,128)(2,1)S(1)} %bitcast.18, bf16[3,96,128,128]{3,2,1,0:T(8,128)(2,1)S(1)} %copy-done.1, f32[8,8,128]{2,1,0:T(8,128)S(1)} %get-tuple-element.17.refs_0_), custom_call_target="tpu_custom_call" | custom-call | flops 5000000000 | bytes 10000000 | tf_op jit(solution)/shard_map/products/pallas_call | solution.py:377
  18.5 0.0 collective-permute-done.1
  18.5 3.7 %collective-permute-start.2 = (bf16[208,128]{1,0:T(8,128)(2,1)S(1)}, bf16[208,128]{1,0:T(8,128)(2,1)S(1)}, u32[]{:S(2)}, u32[]{:S(2)}) collective-permute-start(bf16[208,128]{1,0:T(8,128)(2,1)S(1)} %pad_maximum_fusion), channel_id=1, source_target_pairs={{0,6},{1,7},{2,4},{3,5},{4,2},{5,3},{6,0},{7,1},{8,14},{9,15},{10,... | collective-permute-start | bytes 159752 | tf_op jit(solution)/shard_map/ppermute | solution.py:417
  22.2 0.0 collective-permute-start.3
  22.2 0.8 %collective-permute-start.4 = (bf16[208,128]{1,0:T(8,128)(2,1)S(1)}, bf16[208,128]{1,0:T(8,128)(2,1)S(1)}, u32[]{:S(2)}, u32[]{:S(2)}) collective-permute-start(bf16[208,128]{1,0:T(8,128)(2,1)S(1)} %pad_maximum_fusion.2), channel_id=1, source_target_pairs={{0,2},{1,3},{2,0},{3,1},{4,6},{5,7},{6,4},{7,5},{8,10},{9,11},{10,... | collective-permute-start | bytes 159752 | tf_op jit(solution)/shard_map/ppermute | solution.py:417
  23.0 0.0 collective-permute-done.partner_ref
  23.0 0.2 own.1
  23.2 1.4 %collective-permute-done.2.refs_0_ = bf16[208,128]{1,0:T(8,128)(2,1)S(1)} collective-permute-done((bf16[208,128]{1,0:T(8,128)(2,1)S(1)}, bf16[208,128]{1,0:T(8,128)(2,1)S(1)}, u32[]{:S(2)}, u32[]{:S(2)}) %collective-permute-start.2) | collective-permute-done | bytes 53280 | tf_op jit(solution)/shard_map/ppermute | solution.py:417
  24.7 2.8 %collective-permute-done.3.refs_1_ = bf16[208,128]{1,0:T(8,128)(2,1)S(1)} collective-permute-done((bf16[208,128]{1,0:T(8,128)(2,1)S(1)}, bf16[208,128]{1,0:T(8,128)(2,1)S(1)}, u32[]{:S(2)}, u32[]{:S(2)}) %collective-permute-start.3) | collective-permute-done | bytes 53280 | tf_op jit(solution)/shard_map/ppermute | solution.py:417
  27.5 0.1 collective-permute-done.4.refs_2_
  27.6 0.0 copy-done
  27.6 1.0 %merge.1 = (f32[8,4096]{1,0:T(8,128)S(1)}, f32[32,4,128]{2,1,0:T(4,128)S(1)}) custom-call(bf16[40,4096]{1,0:T(8,128)(2,1)S(1)} %copy-done, f32[256,128]{1,0:T(8,128)S(1)} %get-tuple-element.20.total_ref, f32[8,128]{1,0:T(8,128)S(1)} %get-tuple-element.21.small_ref, bf16[208,128]{1,0:T(8,128)(2,1)S(1)} %collective-permute-done.2.refs_0_, ...), custom_call_target="tpu_custom_call" | custom-call | tf_op jit(solution)/shard_map/merge/pallas_call | solution.py:418
  28.6 10.7 %all_to_all.5.packets_ref = f32[32,4,128]{2,1,0:T(4,128)S(1)} all-to-all(f32[32,4,128]{2,1,0:T(4,128)S(1)} %get-tuple-element.23), channel_id=1, replica_groups=mesh['row'=4,'col'=8] {'row','col'}, dimensions={0} | all-to-all | bytes 131072 | tf_op jit(solution)/shard_map/all_to_all | solution.py:430
  39.2 1.5 %finish.1 = (f32[8,4096]{1,0:T(8,128)}, f32[8,40]{1,0:T(8,128)}, f32[8,8]{1,0:T(8,128)}) custom-call(f32[32,4,128]{2,1,0:T(4,128)S(1)} %all_to_all.5.packets_ref, f32[8,4096]{1,0:T(8,128)S(1)} %get-tuple-element.24.applied_ref, bf16[40,4096]{1,0:T(8,128)(2,1)S(1)} %copy-done), custom_call_target="tpu_custom_call" | custom-call | tf_op jit(solution)/shard_map/finish/pallas_call | solution.py:431
  (5 shorter events, 0.0 us)
Async XLA Ops:
  0.6 14.9 %copy-start.1 = (bf16[3,96,128,128]{3,2,1,0:T(8,128)(2,1)S(1)}, bf16[3,96,128,128]{3,2,1,0:T(8,128)(2,1)}, u32[]{:S(2)}) copy-start(bf16[3,96,128,128]{3,2,1,0:T(8,128)(2,1)} %tiles_ref.5) | copy-start | bytes 28311556
  17.1 5.9 %collective-permute-start = (bf16[1,104,128]{2,1,0:T(8,128)(2,1)S(1)}, bf16[1,104,128]{2,1,0:T(8,128)(2,1)S(1)}, u32[]{:S(2)}, u32[]{:S(2)}) collective-permute-start(bf16[1,104,128]{2,1,0:T(8,128)(2,1)S(1)} %get-tuple-element.19), channel_id=1, source_target_pairs={{0,1},{1,0},{2,3},{3,2},{4,5},{5,4},{6,7},{7,6},{8,9},{9,8},{10,11... | collective-permute-start | bytes 79880 | tf_op jit(solution)/shard_map/ppermute | solution.py:398
  17.1 10.5 %copy-start = (bf16[40,4096]{1,0:T(8,128)(2,1)S(1)}, bf16[40,4096]{1,0:T(8,128)(2,1)}, u32[]{:S(2)}) copy-start(bf16[40,4096]{1,0:T(8,128)(2,1)} %basis_ref.5) | copy-start | bytes 983044
  17.1 1.4 %collective-permute-start.1 = (bf16[3,104,128]{2,1,0:T(8,128)(2,1)S(1)}, bf16[3,104,128]{2,1,0:T(8,128)(2,1)S(1)}, u32[]{:S(2)}, u32[]{:S(2)}) collective-permute-start(bf16[3,104,128]{2,1,0:T(8,128)(2,1)S(1)} %get-tuple-element.22), channel_id=1, source_target_pairs={{0,1},{1,0},{2,3},{3,2},{4,5},{5,4},{6,7},{7,6},{8,9},{9,8},{10,11... | collective-permute-start | bytes 239624 | tf_op jit(solution)/shard_map/ppermute | solution.py:395
  18.5 6.1 %collective-permute-start.2 = (bf16[208,128]{1,0:T(8,128)(2,1)S(1)}, bf16[208,128]{1,0:T(8,128)(2,1)S(1)}, u32[]{:S(2)}, u32[]{:S(2)}) collective-permute-start(bf16[208,128]{1,0:T(8,128)(2,1)S(1)} %pad_maximum_fusion), channel_id=1, source_target_pairs={{0,6},{1,7},{2,4},{3,5},{4,2},{5,3},{6,0},{7,1},{8,14},{9,15},{10,... | collective-permute-start | bytes 159752 | tf_op jit(solution)/shard_map/ppermute | solution.py:417
  22.2 5.3 %collective-permute-start.3 = (bf16[208,128]{1,0:T(8,128)(2,1)S(1)}, bf16[208,128]{1,0:T(8,128)(2,1)S(1)}, u32[]{:S(2)}, u32[]{:S(2)}) collective-permute-start(bf16[208,128]{1,0:T(8,128)(2,1)S(1)} %pad_maximum_fusion.1), channel_id=1, source_target_pairs={{0,4},{1,5},{2,6},{3,7},{4,0},{5,1},{6,2},{7,3},{8,12},{9,13},{10,... | collective-permute-start | bytes 159752 | tf_op jit(solution)/shard_map/ppermute | solution.py:417
  22.2 5.3 %collective-permute-start.4 = (bf16[208,128]{1,0:T(8,128)(2,1)S(1)}, bf16[208,128]{1,0:T(8,128)(2,1)S(1)}, u32[]{:S(2)}, u32[]{:S(2)}) collective-permute-start(bf16[208,128]{1,0:T(8,128)(2,1)S(1)} %pad_maximum_fusion.2), channel_id=1, source_target_pairs={{0,2},{1,3},{2,0},{3,1},{4,6},{5,7},{6,4},{7,5},{8,10},{9,11},{10,... | collective-permute-start | bytes 159752 | tf_op jit(solution)/shard_map/ppermute | solution.py:417

commit v3 on v2

--- a/solution.py
+++ b/solution.py
@@ -26,9 +26,9 @@
 
 
 def series_kernel(
-    region, tile, basis_ref, expand_ref, cols_ref, rows_ref, out_ref, *refs
+    region, tile, basis_ref, expand_ref, cols_ref, rows_ref, out_ref, local_ref, *refs
 ):
-    tables, (scratch, here, small, lists, sems) = refs[:2], refs[2:]
+    tables, (here, small, lists, sems) = refs[:2], refs[2:]
     rows, krylov = expand_ref.shape
     groups = basis_ref.shape[0] // 8
     copies = [pltpu.make_async_copy(expand_ref, small, sems.at[groups])]
@@ -39,7 +39,7 @@
         copies.append(pltpu.make_async_copy(basis_ref.at[part], here.at[part], sems.at[g]))
     for copy in copies:
         copy.start()
-    scratch[...] = jnp.zeros_like(scratch)
+    local_ref[...] = jnp.zeros_like(local_ref)
     for copy in copies:
         copy.wait()
     basis = here[...]
@@ -48,43 +48,32 @@
     series = (wide[:rows] + wide[rows:]).astype(BF16)
     for t in range(region):
         out_ref[t] = series[:, t * tile : (t + 1) * tile]
-    local = contract_lanes(basis, basis)
-    high = local.astype(BF16).astype(F32)
-    low = local - high
-    rest = krylov - rows
-    corner = 2 * krylov
-    scratch[:, :krylov] = high[:rows]
-    scratch[:, krylov:corner] = low[:rows]
-    scratch[:rest, corner : corner + rest] = high[rows:, rows:]
-    scratch[:rest, corner + rest : corner + 2 * rest] = low[rows:, rows:]
-    out_ref[region] = scratch[...].astype(BF16)
+    krylov = basis.shape[0]
+    local_ref[:, :krylov] = contract_lanes(basis, basis)
     for k, table in enumerate(tables):
         spread = jnp.broadcast_to(lists[k].astype(F32), (tile, lists.shape[2]))
         table[...] = spread.T.astype(jnp.int32)
 
 
-def share_correlation(sizes, gathered_ref, scratch, slices):
-    row_count, region, krylov, _, _, share = sizes
-    rows, _ = gathered_ref.shape[2:]
-    rest = krylov - rows
-    corner = 2 * krylov
-    total = gathered_ref[0, region].astype(F32)
-    for r in range(1, row_count):
-        total += gathered_ref[r, region].astype(F32)
-    top = total[:, :krylov] + total[:, krylov:corner]
-    square = (total[:, corner : corner + rest] + total[:, corner + rest : corner + 2 * rest])[:rest]
-    scratch[...] = jnp.zeros_like(scratch)
-    scratch[:rows, :krylov] = top
-    scratch[rows:krylov, :rows] = top.T[rows:krylov]
-    scratch[rows:krylov, rows:krylov] = square
-    merged = scratch[:krylov, :krylov]
-    high = merged.astype(BF16).astype(F32)
-    scratch[:krylov, :krylov] = high
-    scratch[:krylov, HALF : HALF + krylov] = merged - high
-    slices[...] = jnp.zeros_like(slices)
-    for c in range(slices.shape[0]):
-        if c * share < krylov:
-            slices[c, :share, :] = scratch[c * share : (c + 1) * share, :]
+def upper_blocks(krylov):
+    count = krylov // 8
+    return [(i, j) for i in range(count) for j in range(i, count)]
+
+
+def share_blocks(start, turn, local_ref, table_ref):
+    krylov, tile = local_ref.shape
+    lane = lax.broadcasted_iota(jnp.int32, (8, tile), 1)
+    pairs = upper_blocks(krylov)
+    for c in range(table_ref.shape[1]):
+        value = jnp.zeros((8, tile), F32)
+        for k, (i, j) in enumerate(pairs[2 * c : 2 * c + 2]):
+            target = start + 8 * k
+            moved = pltpu.roll(local_ref[8 * i : 8 * i + 8, :], (target - 8 * j) % tile, 1)
+            value = jnp.where((lane >= target) & (lane < target + 8), moved, value)
+        high = value.astype(BF16).astype(F32)
+        both = high + pltpu.roll(value - high, 16, 1)
+        table_ref[0, c] = both
+        table_ref[1, c] = pltpu.roll(both, turn, 1)
 
 
 def placed(piece, code, place):
@@ -95,16 +84,15 @@
 def tile_kernel(sizes, groups, first, cols_ref, rows_ref, gathered_ref, tiles_ref, *refs):
     refs, turned = refs[:-1], refs[-1]
     used = []
-    _, region, _, cap, vectors, _ = sizes
+    region, cap, vectors = sizes
     tile = tiles_ref.shape[2]
     span = (cap + 1) * vectors
     position = lax.axis_index("col")
     if first:
-        slices, scratch = refs[-2:]
-        out_refs = refs[:-2]
-        share_correlation(sizes, gathered_ref, scratch, slices)
+        local_ref, out_refs, table = refs[0], refs[1:-1], refs[-1]
+        share_blocks(cap * vectors, span, local_ref, table)
     else:
-        slices, out_refs = refs[0], refs[1:]
+        table, out_refs = refs[0], refs[1:]
     lane = lax.broadcasted_iota(jnp.int32, (8, tile), 1)
     sublane = lax.broadcasted_iota(jnp.int32, (8, tile), 0)
 
@@ -161,7 +149,8 @@
             code = jnp.where(
                 slot == s, (rows_ref[pl.ds(base + s, 1), :] - target * region) * vectors + inner, code
             )
-        last = jnp.where(sublane == 7, code.astype(F32), slices[target])
+        coded = (sublane == 7) & (slot < cap)
+        last = jnp.where(coded, code.astype(F32), table[core, target])
         out_ref[place, cap * vectors : (cap + 1) * vectors, :] = last.astype(BF16)
 
     for group, out_ref in zip(groups, out_refs):
@@ -170,27 +159,30 @@
 
 
 def own_kernel(sizes, own_ref, partner_ref, total_ref, small_ref):
-    _, _, _, cap, vectors, _ = sizes
+    _, cap, vectors = sizes
     tile = total_ref.shape[1]
     span = (cap + 1) * vectors
     place = lax.broadcasted_iota(jnp.int32, total_ref.shape, 0).astype(F32)
     total = jnp.zeros(total_ref.shape, F32)
     small = jnp.zeros(small_ref.shape, F32)
+    row_lane = lax.broadcasted_iota(jnp.int32, (1, tile), 1)
     for piece, shift in ((own_ref[0], 0), (partner_ref[0], tile - span)):
         last = piece[cap * vectors :].astype(F32)
+        last = pltpu.roll(last, shift, 1) if shift else last
         small += last
-        code = pltpu.roll(last, shift, 1) if shift else last
-        total += placed(piece, code[7:8, :], place)
+        code = jnp.where(row_lane < cap * vectors, last[7:8, :], -1.0)
+        total += placed(piece, code, place)
     total_ref[...] = total
     small_ref[...] = small
 
 
 def merge_kernel(sizes, basis_ref, total_ref, small_ref, *refs):
-    region, krylov, cap, vectors, each = sizes
-    blocks, (applied_ref, packet_ref, scratch) = refs[:-3], refs[-3:]
+    region, krylov, cap, vectors = sizes
+    blocks, (applied_ref, packet_ref) = refs[:-2], refs[-2:]
     tile = applied_ref.shape[1] // region
     total = total_ref[...]
     small = small_ref[...]
+    turned = jnp.zeros_like(small)
     place = lax.broadcasted_iota(jnp.int32, (region * vectors, 2 * tile), 0).astype(F32)
     span = (cap + 1) * vectors
     row_lane = lax.broadcasted_iota(jnp.int32, (1, tile), 1)
@@ -198,9 +190,12 @@
         piece = ref[...]
         near = piece[cap * vectors : span].astype(F32)
         far = piece[span + cap * vectors :].astype(F32)
-        small += near + far
-        code = jnp.where(row_lane < span, near[7:8, :], far[7:8, :])
-        total += placed(piece, jnp.concatenate([code, far[7:8, :]], axis=1), place)
+        small += near
+        turned += far
+        near_code = jnp.where(row_lane < cap * vectors, near[7:8, :], -1.0)
+        far_code = jnp.where(lax.rem(row_lane + tile - span, tile) < cap * vectors, far[7:8, :], -1.0)
+        code = jnp.where(row_lane < span, near_code, far_code)
+        total += placed(piece, jnp.concatenate([code, far_code], axis=1), place)
     for t in range(region):
         applied_ref[:, t * tile : (t + 1) * tile] = total[t * vectors : (t + 1) * vectors]
     applied = applied_ref[...]
@@ -212,22 +207,13 @@
     energy = (cross[:vectors, :vectors] + cross[vectors:, vectors:]) + (
         cross[:vectors, vectors:] + cross[vectors:, :vectors]
     )
-    low_half = pltpu.roll(small, tile - HALF, 1)
+    small += pltpu.roll(turned, tile - span, 1)
+    small += pltpu.roll(small, tile - 16, 1)
     lane = lax.broadcasted_iota(jnp.int32, (vectors, tile), 1)
-    sublane = lax.broadcasted_iota(jnp.int32, (vectors, tile), 0)
-    scratch[...] = jnp.zeros_like(scratch)
-    scratch[:vectors, :] = jnp.where(lane < krylov, small + low_half, 0.0)
     used = krylov + vectors
-    width = HALF - used
     packet = jnp.concatenate([raw, energy, jnp.zeros((vectors, tile - used), F32)], axis=1)
-    first_row = lax.axis_index("row") * each
-    pieces = -(-krylov // width)
-    for i in range(each):
-        row = scratch[pl.ds(first_row + i, 1), :]
-        for p in range(pieces):
-            moved = pltpu.roll(row, (used - p * width) % tile, 1)
-            here = (sublane == i * pieces + p) & (lane >= used) & (lane < HALF)
-            packet = jnp.where(here, moved, packet)
+    moved = pltpu.roll(small, (HALF - 16 - cap * vectors) % tile, 1)
+    packet = jnp.where((lane >= HALF - 16) & (lane < HALF), moved, packet)
     folded = jnp.where(
         lane[: vectors // 2] < HALF,
         packet[: vectors // 2],
@@ -243,34 +229,37 @@
 
 
 def finish_kernel(
-    sizes, packets_ref, applied_ref, basis_ref, new_ref, coefficients_ref, factor_ref, scratch
+    sizes, packets_ref, applied_ref, basis_ref, new_ref, coefficients_ref, factor_ref
 ):
-    krylov, vectors, share, each, col_count, entries = sizes
+    krylov, vectors, col_count, entries = sizes
     inverse_root = 1.0 / math.sqrt(entries)
-    devices, half, tile = packets_ref.shape
-    folded = tree_sum([packets_ref[d] for d in range(devices)])
+    devices, _, tile = packets_ref.shape
+    row_count = devices // col_count
+    shares = [
+        tree_sum([packets_ref[r * col_count + c] for r in range(row_count)])
+        for c in range(col_count)
+    ]
+    folded = tree_sum(shares)
     total = jnp.concatenate([folded, pltpu.roll(folded, HALF, 1)], axis=0)
-    used = krylov + vectors
-    width = HALF - used
-    pieces = -(-krylov // width)
-    lanes = lax.broadcasted_iota(jnp.int32, (devices, tile), 1)
-    for i in range(each):
-        found = jnp.zeros((devices, tile), F32)
-        for p in range(pieces):
-            n = i * pieces + p
-            start = used + (n // half) * HALF
-            moved = pltpu.roll(packets_ref[:, n % half, :], (p * width - start) % tile, 1)
-            found = jnp.where((lanes >= p * width) & (lanes < (p + 1) * width), moved, found)
-        for d in range(devices):
-            r, c = divmod(d, col_count)
-            row = c * share + r * each + i
-            if r * each + i < share and row < krylov:
-                scratch[row : row + 1, :] = found[d : d + 1]
-    correlation = scratch[:krylov, :krylov] * (1.0 / entries)
+    lane = lax.broadcasted_iota(jnp.int32, (vectors, tile), 1)
+    zero = jnp.zeros((vectors, tile), F32)
+    upper = [zero] * (krylov // 8)
+    strict = [zero] * (krylov // 8)
+    for n, (i, j) in enumerate(upper_blocks(krylov)):
+        part = shares[n // 2] * (1.0 / entries)
+        part = jnp.concatenate([part, pltpu.roll(part, HALF, 1)], axis=0)
+        moved = pltpu.roll(part, (8 * j - (HALF - 16) - 8 * (n % 2)) % tile, 1)
+        here = (lane >= 8 * j) & (lane < 8 * j + 8)
+        upper[i] = jnp.where(here, moved, upper[i])
+        if i < j:
+            strict[i] = jnp.where(here, moved, strict[i])
+    upper = jnp.concatenate(upper, axis=0)[:, :krylov]
+    strict = jnp.concatenate(strict, axis=0)[:, :krylov]
     first = total[:, :krylov] * inverse_root
     energy = total[:, krylov : krylov + vectors]
-    corr_high = correlation.astype(BF16)
-    corr_low = (correlation - corr_high.astype(F32)).astype(BF16)
+    upper_high, strict_high = upper.astype(BF16), strict.astype(BF16)
+    upper_low = (upper - upper_high.astype(F32)).astype(BF16)
+    strict_low = (strict - strict_high.astype(F32)).astype(BF16)
 
     def halves(value):
         high = value.astype(BF16).astype(F32)
@@ -278,8 +267,10 @@
 
     def times_correlation(value):
         high, both = halves(value)
-        main = jnp.dot(both, corr_high, preferred_element_type=F32)
-        rest = jnp.dot(high, corr_low, preferred_element_type=F32)
+        main = jnp.dot(both, upper_high, preferred_element_type=F32)
+        main += contract_lanes(both, strict_high)
+        rest = jnp.dot(high, upper_low, preferred_element_type=F32)
+        rest += contract_lanes(high, strict_low)
         return main[:vectors] + (main[vectors:] + rest)
 
     coefficients = first + (first - times_correlation(first))
@@ -325,28 +316,26 @@
     devices = row_count * col_count
     entries = length * devices
     cap = tiles.shape[1] // col_count
-    share = -(-krylov // col_count)
-    each = -(-share // row_count)
     span = (cap + 1) * vectors
-    assert krylov + vectors < HALF and share < 8 and region * vectors <= 256
-    assert each * -(-krylov // (HALF - krylov - vectors)) <= vectors and cap % 2 == 0
-    assert rows < krylov <= 2 * rows and 4 * krylov - 2 * rows <= tile
+    assert krylov % 8 == 0 and krylov + vectors <= HALF - 16 and tile == 2 * HALF
+    assert len(upper_blocks(krylov)) <= 2 * col_count and region * vectors <= 256
+    assert vectors == 8 and cap % 2 == 0 and cap * vectors + 32 <= tile
     vmem = pl.BlockSpec(memory_space=pltpu.VMEM)
     hbm = pl.BlockSpec(memory_space=pltpu.HBM)
 
     count = tile_cols.shape[0]
     index_table = jax.ShapeDtypeStruct((count, tile), jnp.int32)
-    series, wide_cols, wide_rows = pl.pallas_call(
+    series, local, wide_cols, wide_rows = pl.pallas_call(
         functools.partial(series_kernel, region, tile),
         out_shape=(
-            jax.ShapeDtypeStruct((region + 1, rows, tile), BF16),
+            jax.ShapeDtypeStruct((region, rows, tile), BF16),
+            jax.ShapeDtypeStruct((krylov, tile), F32),
             index_table,
             index_table,
         ),
         in_specs=[hbm] * 4,
-        out_specs=(vmem,) * 3,
+        out_specs=(vmem,) * 4,
         scratch_shapes=[
-            pltpu.VMEM((rows, tile), F32),
             pltpu.VMEM(basis.shape, BF16),
             pltpu.VMEM((rows, krylov), F32),
             pltpu.VMEM((2, 1, count), jnp.int32),
@@ -368,33 +357,31 @@
     )
     gathered = lax.all_gather(series, "row", axis=0)
     half = col_count // 2
-    sizes = (row_count, region, krylov, cap, vectors, share)
-
-    def products(groups, *slices):
-        first = not slices
+    sizes = (region, cap, vectors)
+
+    def products(groups, given, first=False):
         shapes = [((len(group), span, tile), BF16) for group in groups]
-        shapes += [((col_count, 8, tile), F32)] * first
+        shapes += [((2, col_count, 8, tile), F32)] * first
+        weights = 9 * sum(map(len, groups))
         return pl.pallas_call(
             functools.partial(tile_kernel, sizes, groups, first),
             out_shape=tuple(jax.ShapeDtypeStruct(*shape) for shape in shapes),
-            in_specs=[vmem] * (4 + len(slices)),
+            in_specs=[vmem] * 5,
             out_specs=(vmem,) * len(shapes),
-            scratch_shapes=[pltpu.VMEM((max(krylov, share * col_count), tile), F32)] * first
-            + [pltpu.VMEM((9 * max(1, sum(map(len, groups))), 2 * tile, 2 * tile), BF16)],
+            scratch_shapes=[pltpu.VMEM((weights, 2 * tile, 2 * tile), BF16)],
             cost_estimate=pl.CostEstimate(
                 flops=5 * 10**9, bytes_accessed=10**7, transcendentals=0
             ),
             compiler_params=pltpu.CompilerParams(vmem_limit_bytes=16 << 20),
             name="products",
-        )(wide_cols, wide_rows, gathered, tiles, *slices)
+        )(wide_cols, wide_rows, gathered, tiles, given)
 
     apart = tuple(range(half - 1, 0, -1))
-    far = apart
     swap = [(i, i ^ 1) for i in range(col_count)]
-    other, slices = products((tuple((1, d) for d in apart),))
+    other, table = products((tuple((1, d) for d in apart),), local, True)
     partner = lax.ppermute(other, "col", swap)
-    (mine_far,) = products((tuple((0, d) for d in far),), slices)
-    other_here, own = products((((1, 0),), ((0, 0),)), slices)
+    (mine,) = products((tuple((0, d) for d in apart),), table)
+    other_here, own = products((((1, 0),), ((0, 0),)), table)
     partner_here = lax.ppermute(other_here, "col", swap)
     blocks = list(
         pl.pallas_call(
@@ -410,26 +397,24 @@
             name="own",
         )(own, partner_here)
     )
-    for distances, mine in ((far, mine_far),):
-        for place, distance in enumerate(distances):
-            moves = [(i, i ^ (2 * distance)) for i in range(col_count)]
-            pair = jnp.concatenate([mine[place], partner[apart.index(distance)]], axis=0)
-            blocks.append(lax.ppermute(pair, "col", moves))
+    for place, distance in enumerate(apart):
+        moves = [(i, i ^ (2 * distance)) for i in range(col_count)]
+        pair = jnp.concatenate([mine[place], partner[place]], axis=0)
+        blocks.append(lax.ppermute(pair, "col", moves))
     applied, packet = pl.pallas_call(
-        functools.partial(merge_kernel, (region, krylov, cap, vectors, each)),
+        functools.partial(merge_kernel, (region, krylov, cap, vectors)),
         out_shape=(
             jax.ShapeDtypeStruct((vectors, length), F32),
             jax.ShapeDtypeStruct((devices, vectors // 2, tile), F32),
         ),
         in_specs=[vmem] * (1 + len(blocks)),
         out_specs=(vmem, vmem),
-        scratch_shapes=[pltpu.VMEM((max(8, row_count * each), tile), F32)],
         compiler_params=pltpu.CompilerParams(vmem_limit_bytes=8 << 20),
         name="merge",
     )(basis, *blocks)
     packets = lax.all_to_all(packet, ("row", "col"), 0, 0, tiled=True)
     return pl.pallas_call(
-        functools.partial(finish_kernel, (krylov, vectors, share, each, col_count, entries)),
+        functools.partial(finish_kernel, (krylov, vectors, col_count, entries)),
         out_shape=(
             jax.ShapeDtypeStruct((vectors, length), F32),
             jax.ShapeDtypeStruct((vectors, krylov), F32),
@@ -437,7 +422,6 @@
         ),
         in_specs=[vmem] * 3,
         out_specs=(vmem,) * 3,
-        scratch_shapes=[pltpu.VMEM((share * col_count, tile), F32)],
         compiler_params=pltpu.CompilerParams(vmem_limit_bytes=4 << 20),
         name="finish",
     )(packets, applied, basis)

time: 40.9 us -> 40.7 us (level)
  no operation moved by 1% of the time
where the time goes in v3:
time: 40.7 us; the launch traced here: 40.5 us
  blocking collectives  23.6 us (58%)
  Pallas kernels  6.81 us (17%)
  starting transfers between devices  4.96 us (12%)
  waiting for transfers between devices  4.38 us (11%)
  between operations  0.7 us (2%)
    all_gather x1, blocking collectives, shards(): gathered = lax.all_gather(series, 'row', axis=0)  12.9 us
    all_to_all x1, blocking collectives, shards(): packets = lax.all_to_all(packet, ('row', 'col'), 0, 0, tiled=True)  10.7 us
    ppermute x3, starting transfers between devices, shards(): blocks.append(lax.ppermute(pair, 'col', moves))  4.44 us
    ppermute x3, waiting for transfers between devices, shards(): blocks.append(lax.ppermute(pair, 'col', moves))  4.34 us
    pallas_call x3, Pallas kernels, products(): pl.pallas_call(functools.partial(tile_kernel, sizes, groups, first), out_...  2.42 us
    pallas_call x1, Pallas kernels, shards(): pl.pallas_call(functools.partial(finish_kernel, (krylov, vectors, col_cou...  1.63 us
    pallas_call x1, Pallas kernels, shards(): pl.pallas_call(functools.partial(series_kernel, region, tile), out_shape=...  1.58 us
    pallas_call x1, Pallas kernels, shards(): pl.pallas_call(functools.partial(merge_kernel, (region, krylov, cap, vect...  0.96 us
  transfers between devices with their start and end apart: 5, of which 3 were waited for; matrix products, arithmetic and copies ran while one was open for 0% of the time, Pallas kernels for 3%

profile of v3, /device:TPU:0, one launch (start us, length us, event | category | flops | bytes accessed | tf_op | source)
XLA Modules:
  0.0 40.5 jit_solution(1390521198930288489)
XLA Ops:
  0.6 0.0 copy-start.1
  0.6 1.6 %series.1 = (bf16[32,24,128]{2,1,0:T(8,128)(2,1)S(1)}, f32[40,128]{1,0:T(8,128)S(1)}, s32[96,128]{1,0:T(8,128)S(1)}, s32[96,128]{1,0:T(8,128)S(1)}) custom-call(bf16[40,4096]{1,0:T(8,128)(2,1)} %basis_ref.5, f32[24,40]{1,0:T(8,128)} %bitcast.19, s32[1,96]{1,0:T(1,128)} %bitcast.20, s32[1,96]{1,0:T(1,128)} %bitcast.21), custom_call_target="tpu_custom_call" | custom-call | flops 10000000000 | bytes 10000000 | tf_op jit(solution)/shard_map/series/pallas_call | solution.py:328
  2.2 12.9 %all-gather = bf16[128,24,128]{2,1,0:T(8,128)(2,1)S(1)} all-gather(bf16[32,24,128]{2,1,0:T(8,128)(2,1)S(1)} %get-tuple-element.17), channel_id=2, replica_groups=mesh['row'=4,'col'=8] {'row'}, dimensions={0}, use_global_device_ids=true | all-gather | bytes 983040 | tf_op jit(solution)/shard_map/all_gather | solution.py:358
  15.2 0.0 copy-done.1
  15.2 0.9 %products.3 = (bf16[3,104,128]{2,1,0:T(8,128)(2,1)S(1)}, f32[2,8,8,128]{3,2,1,0:T(8,128)S(1)}) custom-call(s32[96,128]{1,0:T(8,128)S(1)} %get-tuple-element.15.cols_ref, s32[96,128]{1,0:T(8,128)S(1)} %get-tuple-element.16.rows_ref, bf16[4,32,24,128]{3,2,1,0:T(8,128)(2,1)S(1)} %bitcast.16, bf16[3,96,128,128]{3,2,1,0:T(8,128)(2,1)S(1)} %copy-done.1, ...), custom_call_target="tpu_custom_call" | custom-call | flops 5000000000 | bytes 10000000 | tf_op jit(solution)/shard_map/products/pallas_call | solution.py:366
  16.1 0.6 %products.4 = (bf16[1,104,128]{2,1,0:T(8,128)(2,1)S(1)}, bf16[1,104,128]{2,1,0:T(8,128)(2,1)S(1)}) custom-call(s32[96,128]{1,0:T(8,128)S(1)} %get-tuple-element.15.cols_ref, s32[96,128]{1,0:T(8,128)S(1)} %get-tuple-element.16.rows_ref, bf16[4,32,24,128]{3,2,1,0:T(8,128)(2,1)S(1)} %bitcast.17, bf16[3,96,128,128]{3,2,1,0:T(8,128)(2,1)S(1)} %copy-done.1, ...), custom_call_target="tpu_custom_call" | custom-call | flops 5000000000 | bytes 10000000 | tf_op jit(solution)/shard_map/products/pallas_call | solution.py:366
  16.7 0.0 collective-permute-start
  16.7 0.0 copy-start
  16.7 0.5 %collective-permute-start.1 = (bf16[3,104,128]{2,1,0:T(8,128)(2,1)S(1)}, bf16[3,104,128]{2,1,0:T(8,128)(2,1)S(1)}, u32[]{:S(2)}, u32[]{:S(2)}) collective-permute-start(bf16[3,104,128]{2,1,0:T(8,128)(2,1)S(1)} %get-tuple-element.24), channel_id=1, source_target_pairs={{0,1},{1,0},{2,3},{3,2},{4,5},{5,4},{6,7},{7,6},{8,9},{9,8},{10,11... | collective-permute-start | bytes 239624 | tf_op jit(solution)/shard_map/ppermute | solution.py:382
  17.3 0.9 %products.5 = bf16[3,104,128]{2,1,0:T(8,128)(2,1)S(1)} custom-call(s32[96,128]{1,0:T(8,128)S(1)} %get-tuple-element.15.cols_ref, s32[96,128]{1,0:T(8,128)S(1)} %get-tuple-element.16.rows_ref, bf16[4,32,24,128]{3,2,1,0:T(8,128)(2,1)S(1)} %bitcast.18, bf16[3,96,128,128]{3,2,1,0:T(8,128)(2,1)S(1)} %copy-done.1, f32[2,8,8,128]{3,2,1,0:T(8,128)S(1)} %get-tuple-element.19.refs_0_), custom_call_target="tpu_custom_call" | custom-call | flops 5000000000 | bytes 10000000 | tf_op jit(solution)/shard_map/products/pallas_call | solution.py:366
  18.1 0.0 collective-permute-done.1
  18.2 3.7 %collective-permute-start.2 = (bf16[208,128]{1,0:T(8,128)(2,1)S(1)}, bf16[208,128]{1,0:T(8,128)(2,1)S(1)}, u32[]{:S(2)}, u32[]{:S(2)}) collective-permute-start(bf16[208,128]{1,0:T(8,128)(2,1)S(1)} %pad_maximum_fusion), channel_id=1, source_target_pairs={{0,6},{1,7},{2,4},{3,5},{4,2},{5,3},{6,0},{7,1},{8,14},{9,15},{10,... | collective-permute-start | bytes 159752 | tf_op jit(solution)/shard_map/ppermute | solution.py:403
  21.9 0.0 collective-permute-start.3
  21.9 0.8 %collective-permute-start.4 = (bf16[208,128]{1,0:T(8,128)(2,1)S(1)}, bf16[208,128]{1,0:T(8,128)(2,1)S(1)}, u32[]{:S(2)}, u32[]{:S(2)}) collective-permute-start(bf16[208,128]{1,0:T(8,128)(2,1)S(1)} %pad_maximum_fusion.2), channel_id=1, source_target_pairs={{0,2},{1,3},{2,0},{3,1},{4,6},{5,7},{6,4},{7,5},{8,10},{9,11},{10,... | collective-permute-start | bytes 159752 | tf_op jit(solution)/shard_map/ppermute | solution.py:403
  22.7 0.0 collective-permute-done.partner_ref
  22.7 0.2 own.1
  22.9 1.4 %collective-permute-done.2.refs_0_ = bf16[208,128]{1,0:T(8,128)(2,1)S(1)} collective-permute-done((bf16[208,128]{1,0:T(8,128)(2,1)S(1)}, bf16[208,128]{1,0:T(8,128)(2,1)S(1)}, u32[]{:S(2)}, u32[]{:S(2)}) %collective-permute-start.2) | collective-permute-done | bytes 53280 | tf_op jit(solution)/shard_map/ppermute | solution.py:403
  24.3 2.8 %collective-permute-done.3.refs_1_ = bf16[208,128]{1,0:T(8,128)(2,1)S(1)} collective-permute-done((bf16[208,128]{1,0:T(8,128)(2,1)S(1)}, bf16[208,128]{1,0:T(8,128)(2,1)S(1)}, u32[]{:S(2)}, u32[]{:S(2)}) %collective-permute-start.3) | collective-permute-done | bytes 53280 | tf_op jit(solution)/shard_map/ppermute | solution.py:403
  27.1 0.1 collective-permute-done.4.refs_2_
  27.2 0.0 copy-done
  27.2 1.0 %merge.1 = (f32[8,4096]{1,0:T(8,128)S(1)}, f32[32,4,128]{2,1,0:T(4,128)S(1)}) custom-call(bf16[40,4096]{1,0:T(8,128)(2,1)S(1)} %copy-done, f32[256,128]{1,0:T(8,128)S(1)} %get-tuple-element.22.total_ref, f32[8,128]{1,0:T(8,128)S(1)} %get-tuple-element.23.small_ref, bf16[208,128]{1,0:T(8,128)(2,1)S(1)} %collective-permute-done.2.refs_0_, ...), custom_call_target="tpu_custom_call" | custom-call | tf_op jit(solution)/shard_map/merge/pallas_call | solution.py:404
  28.2 10.7 %all_to_all.5.packets_ref = f32[32,4,128]{2,1,0:T(4,128)S(1)} all-to-all(f32[32,4,128]{2,1,0:T(4,128)S(1)} %get-tuple-element.25), channel_id=1, replica_groups=mesh['row'=4,'col'=8] {'row','col'}, dimensions={0} | all-to-all | bytes 131072 | tf_op jit(solution)/shard_map/all_to_all | solution.py:415
  38.9 1.6 %finish.1 = (f32[8,4096]{1,0:T(8,128)}, f32[8,40]{1,0:T(8,128)}, f32[8,8]{1,0:T(8,128)}) custom-call(f32[32,4,128]{2,1,0:T(4,128)S(1)} %all_to_all.5.packets_ref, f32[8,4096]{1,0:T(8,128)S(1)} %get-tuple-element.26.applied_ref, bf16[40,4096]{1,0:T(8,128)(2,1)S(1)} %copy-done), custom_call_target="tpu_custom_call" | custom-call | tf_op jit(solution)/shard_map/finish/pallas_call | solution.py:416
  (5 shorter events, 0.0 us)
Async XLA Ops:
  0.6 14.5 %copy-start.1 = (bf16[3,96,128,128]{3,2,1,0:T(8,128)(2,1)S(1)}, bf16[3,96,128,128]{3,2,1,0:T(8,128)(2,1)}, u32[]{:S(2)}) copy-start(bf16[3,96,128,128]{3,2,1,0:T(8,128)(2,1)} %tiles_ref.5) | copy-start | bytes 28311556
  16.7 5.9 %collective-permute-start = (bf16[1,104,128]{2,1,0:T(8,128)(2,1)S(1)}, bf16[1,104,128]{2,1,0:T(8,128)(2,1)S(1)}, u32[]{:S(2)}, u32[]{:S(2)}) collective-permute-start(bf16[1,104,128]{2,1,0:T(8,128)(2,1)S(1)} %get-tuple-element.21), channel_id=1, source_target_pairs={{0,1},{1,0},{2,3},{3,2},{4,5},{5,4},{6,7},{7,6},{8,9},{9,8},{10,11... | collective-permute-start | bytes 79880 | tf_op jit(solution)/shard_map/ppermute | solution.py:385
  16.7 10.5 %copy-start = (bf16[40,4096]{1,0:T(8,128)(2,1)S(1)}, bf16[40,4096]{1,0:T(8,128)(2,1)}, u32[]{:S(2)}) copy-start(bf16[40,4096]{1,0:T(8,128)(2,1)} %basis_ref.5) | copy-start | bytes 983044
  16.7 1.4 %collective-permute-start.1 = (bf16[3,104,128]{2,1,0:T(8,128)(2,1)S(1)}, bf16[3,104,128]{2,1,0:T(8,128)(2,1)S(1)}, u32[]{:S(2)}, u32[]{:S(2)}) collective-permute-start(bf16[3,104,128]{2,1,0:T(8,128)(2,1)S(1)} %get-tuple-element.24), channel_id=1, source_target_pairs={{0,1},{1,0},{2,3},{3,2},{4,5},{5,4},{6,7},{7,6},{8,9},{9,8},{10,11... | collective-permute-start | bytes 239624 | tf_op jit(solution)/shard_map/ppermute | solution.py:382
  18.2 6.1 %collective-permute-start.2 = (bf16[208,128]{1,0:T(8,128)(2,1)S(1)}, bf16[208,128]{1,0:T(8,128)(2,1)S(1)}, u32[]{:S(2)}, u32[]{:S(2)}) collective-permute-start(bf16[208,128]{1,0:T(8,128)(2,1)S(1)} %pad_maximum_fusion), channel_id=1, source_target_pairs={{0,6},{1,7},{2,4},{3,5},{4,2},{5,3},{6,0},{7,1},{8,14},{9,15},{10,... | collective-permute-start | bytes 159752 | tf_op jit(solution)/shard_map/ppermute | solution.py:403
  21.9 5.3 %collective-permute-start.3 = (bf16[208,128]{1,0:T(8,128)(2,1)S(1)}, bf16[208,128]{1,0:T(8,128)(2,1)S(1)}, u32[]{:S(2)}, u32[]{:S(2)}) collective-permute-start(bf16[208,128]{1,0:T(8,128)(2,1)S(1)} %pad_maximum_fusion.1), channel_id=1, source_target_pairs={{0,4},{1,5},{2,6},{3,7},{4,0},{5,1},{6,2},{7,3},{8,12},{9,13},{10,... | collective-permute-start | bytes 159752 | tf_op jit(solution)/shard_map/ppermute | solution.py:403
  21.9 5.3 %collective-permute-start.4 = (bf16[208,128]{1,0:T(8,128)(2,1)S(1)}, bf16[208,128]{1,0:T(8,128)(2,1)S(1)}, u32[]{:S(2)}, u32[]{:S(2)}) collective-permute-start(bf16[208,128]{1,0:T(8,128)(2,1)S(1)} %pad_maximum_fusion.2), channel_id=1, source_target_pairs={{0,2},{1,3},{2,0},{3,1},{4,6},{5,7},{6,4},{7,5},{8,10},{9,11},{10,... | collective-permute-start | bytes 159752 | tf_op jit(solution)/shard_map/ppermute | solution.py:403
